TPU v7x, 32 devices: a whole 2x2x4 slice. The times are simulated.
32 devices in a mesh: frame: 4 (over z), space: 8 (over y, x, core).
Axes of the slice: x: 2, y: 2, z: 4, core: 2. Of those that a mesh axis runs over, the one named last changes fastest.
Arguments:
- tokens: bfloat16 [32, 152, 1024], P('space', 'frame'), may hold values from -16 to 16
- tube_count: int32 [8], P('space'), may hold values from 1 to 4, as said below
- ln_gain: float32 [1024], replicated, may hold values from 0.25 to 1.75
- ln_bias: float32 [1024], replicated, may hold values from -3 to 3
- w_qkv: bfloat16 [1024, 1536], replicated, may hold values from -1.5 to 1.5
- w_out: bfloat16 [512, 1024], replicated, may hold values from -0.25 to 0.25
Outputs:
- mixed: bfloat16 [32, 152, 1024], P('space', 'frame')
Inputs may be any that keep to these rules, and one draw needn't show every extreme that they name: tube_count[s] is how many of the 4 slots of space index s hold visible tubes; they are the first ones. Some index has all 4, some only 1.
All inputs are finite; a program needn't handle non-finite values.
Results may differ from a plain program's by a relative error of at most 0.005.
Values may be sent and summed in bfloat16 or wider, within the bound.
No kernel may reach another device: no remote copies, remote signals or barrier semaphores. Data moves between devices by JAX's collectives and lax.ppermute only.
A program may use at most 128 MiB of HBM per device.

v0:
```python
import functools
import jax
import jax.numpy as jnp
from jax import lax
from jax.experimental import pallas as pl
from jax.experimental.pallas import tpu as pltpu
from jax.sharding import Mesh, PartitionSpec as P

HEADS = 8


EPSILON = 1e-06
NEG_FILL = -1e30
LANES = 128
SUBLANES = 8
PACK = 16
SIZE_STEP = 128
SIZE_CASES = 3
MARKS = 2
QUERY_TILE = 256
QUERY_BIG = 512
VMEM_BYTES = 20 * 2**20

VMEM = pl.BlockSpec(memory_space=pltpu.VMEM)
SMEM = pl.BlockSpec(memory_space=pltpu.SMEM)
SWAP = [(0, 1), (1, 0)]


def up_to(value, unit):
    return -(-value // unit) * unit


def params():
    return pltpu.CompilerParams(vmem_limit_bytes=VMEM_BYTES)


def packed_rows(count, slot_rows):
    return (count * slot_rows + PACK - 1) // PACK * PACK


def slot_of(row, slots, slot_rows):
    slot = row * 0
    for edge in range(1, slots):
        slot = slot + (row >= edge * slot_rows).astype(jnp.int32)
    return slot


def live_rows(count, rows, slot_rows, time_dev, width):
    row = lax.broadcasted_iota(jnp.int32, (rows, width), 0)
    slot = slot_of(row, rows // slot_rows, slot_rows)
    return (slot < count) & (row - slot * slot_rows < time_dev)


def one_hot(shape, slots, slot_rows, padded_dim):
    padded = lax.broadcasted_iota(jnp.int32, shape, padded_dim)
    plain = lax.broadcasted_iota(jnp.int32, shape, 1 - padded_dim)
    slot = slot_of(padded, slots, slot_rows)
    hot = plain == (padded - slot * slot_rows) * slots + slot
    return hot.astype(jnp.float32).astype(jnp.bfloat16)


def normalise(x_ref, gain_ref, bias_ref, rows):
    time_dev, slots, width = x_ref.shape
    x = x_ref[...].astype(jnp.float32).reshape(time_dev * slots, width)
    center = x - jnp.mean(x, axis=-1, keepdims=True)
    spread = jnp.mean(center * center, axis=-1, keepdims=True)
    normed = center * lax.rsqrt(spread + EPSILON) * gain_ref[...] + bias_ref[...]
    hot = one_hot((rows, time_dev * slots), slots, rows // slots, 0)
    return jnp.dot(
        hot, normed.astype(jnp.bfloat16), preferred_element_type=jnp.float32
    ).astype(jnp.bfloat16)


def fetch_kernel(
    core_ref,
    x_hbm,
    gain_hbm,
    bias_hbm,
    w_hbm,
    rows_ref,
    gain_ref,
    bias_ref,
    w_ref,
    x_ref,
    sems,
):
    kinds, _, wide = w_ref.shape
    pairs = [(x_hbm, x_ref), (gain_hbm, gain_ref), (bias_hbm, bias_ref)]
    for kind in range(kinds):
        start = pl.multiple_of(2 * wide * kind + wide * core_ref[0], wide)
        pairs.append((w_hbm.at[:, pl.ds(start, wide)], w_ref.at[kind]))
    copies = [
        pltpu.make_async_copy(source, target, sems.at[place])
        for place, (source, target) in enumerate(pairs)
    ]
    for copy in copies:
        copy.start()
    for copy in copies[:-kinds]:
        copy.wait()
    rows_ref[...] = normalise(x_ref, gain_ref, bias_ref, rows_ref.shape[0])
    for copy in copies[-kinds:]:
        copy.wait()


def fetch(core, tokens, ln_gain, ln_bias, w_qkv, rows):
    width = tokens.shape[-1]
    wide = w_qkv.shape[1] // 6
    gain = ln_gain.reshape(1, width)
    bias = ln_bias.reshape(1, width)
    inputs = [pltpu.with_memory_space_constraint(a, pltpu.HBM) for a in (tokens, gain, bias, w_qkv)]
    hbm = pl.BlockSpec(memory_space=pltpu.HBM)
    return pl.pallas_call(
        fetch_kernel,
        out_shape=(
            jax.ShapeDtypeStruct((rows, width), jnp.bfloat16),
            jax.ShapeDtypeStruct(gain.shape, gain.dtype),
            jax.ShapeDtypeStruct(bias.shape, bias.dtype),
            jax.ShapeDtypeStruct((3, width, wide), w_qkv.dtype),
        ),
        in_specs=[SMEM] + [hbm] * 4,
        out_specs=(VMEM,) * 4,
        scratch_shapes=[
            pltpu.VMEM(tokens.shape, tokens.dtype),
            pltpu.SemaphoreType.DMA((6,)),
        ],
        compiler_params=params(),
        cost_estimate=pl.CostEstimate(
            flops=2 * rows * w_qkv.size, bytes_accessed=w_qkv.size, transcendentals=0
        ),
        name="fetch",
    )(core, *inputs)


def project_kernel(
    chip_ref,
    count_ref,
    other_count_ref,
    rows_ref,
    other_ref,
    gain_ref,
    bias_ref,
    w_ref,
    *refs,
):
    chips = len(refs) - 3
    outs = refs[:chips]
    query_ref, key_ref, value_ref = refs[chips:]
    time_dev, slots, _ = other_ref.shape
    message, lanes = outs[0].shape
    rows = message // 3
    slot_rows = rows // slots
    half = rows // 2
    head_size = lanes // 2
    scaling = head_size ** (-0.5)
    chip = chip_ref[0]
    rows_in = jnp.concatenate(
        [rows_ref[...], normalise(other_ref, gain_ref, bias_ref, rows)], axis=0
    )
    for kind, target in enumerate((query_ref, key_ref, value_ref)):
        target[...] = jnp.dot(rows_in, w_ref[kind], preferred_element_type=jnp.float32)
    left = lax.broadcasted_iota(jnp.int32, (rows, lanes), 1) < head_size
    left_half = left[:half]
    row_half = lax.broadcasted_iota(jnp.int32, (half, lanes), 0)
    counts = (count_ref[0], other_count_ref[0])
    flipped = lax.rem(chip, 2) == 1
    for slot in range(chips // 2):
        block = (slot + chip // 2) % (chips // 2) if chips == 4 else slot
        cols = pl.ds(pl.multiple_of(block * lanes, lanes), lanes)
        for group, count in enumerate(counts):
            base = group * rows
            key_pair = key_ref[base : base + rows, cols]
            value_pair = value_ref[base : base + rows, cols]
            live = live_rows(count, rows, slot_rows, time_dev, lanes)
            key_pair = jnp.where(live, key_pair, key_pair[0:1])
            value_pair = jnp.where(live, value_pair, 0.0)
            even = jnp.where(left, key_pair, pltpu.roll(value_pair, head_size, 1))
            odd = jnp.where(left, pltpu.roll(key_pair, head_size, 1), value_pair)
            first = jnp.where(flipped, odd, even).astype(jnp.bfloat16)
            second = jnp.where(flipped, even, odd).astype(jnp.bfloat16)
            outs[2 * slot][base : base + rows] = first
            outs[2 * slot + 1][base : base + rows] = second
            top = query_ref[base : base + half, cols] * scaling
            low = query_ref[base + half : base + rows, cols] * scaling
            even = jnp.where(left_half, top, pltpu.roll(low, head_size, 1))
            odd = jnp.where(left_half, pltpu.roll(top, head_size, 1), low)
            first = jnp.where(flipped, odd, even)
            second = jnp.where(flipped, even, odd)
            if group == 1:
                for index, mark in enumerate(counts):
                    here = (row_half == half - MARKS + index) & jnp.logical_not(left_half)
                    first = jnp.where(here, mark.astype(jnp.float32), first)
                    second = jnp.where(here, mark.astype(jnp.float32), second)
            place = 2 * rows + group * half
            outs[2 * slot][place : place + half] = first.astype(jnp.bfloat16)
            outs[2 * slot + 1][place : place + half] = second.astype(jnp.bfloat16)


def project(chip, count, other_count, rows_in, other_tokens, gain, bias, weights):
    chips = HEADS // 2
    rows = rows_in.shape[0]
    wide = weights.shape[-1]
    held = pltpu.VMEM((2 * rows, wide), jnp.float32)
    message = jax.ShapeDtypeStruct((3 * rows, LANES), jnp.bfloat16)
    return pl.pallas_call(
        project_kernel,
        out_shape=(message,) * chips,
        in_specs=[SMEM] * 3 + [VMEM] * 5,
        out_specs=(VMEM,) * chips,
        scratch_shapes=[held] * 3,
        compiler_params=params(),
        cost_estimate=pl.CostEstimate(
            flops=4 * rows * weights.size, bytes_accessed=2 * weights.size, transcendentals=0
        ),
        name="project",
    )(chip, count, other_count, rows_in, other_tokens, gain, bias, weights)


def source_counts(ref):
    message = ref.shape[0]
    tail = ref[message - PACK : message].astype(jnp.float32)
    return [
        jnp.max(tail[PACK - MARKS + index : PACK - MARKS + index + 1, LANES // 2 :]).astype(jnp.int32)
        for index in range(MARKS)
    ]


def pack_kernel(slot_rows, time_dev, least, cases, *refs):
    got_refs = refs[:-5]
    kv_room, live_room, query_ref, start_ref, case_ref = refs[-5:]
    message, lanes = got_refs[0].shape
    rows = message // 3
    half = rows // 2
    head_size = lanes // 2
    size = live_room.shape[0] - rows
    lane = lax.broadcasted_iota(jnp.int32, (PACK, lanes), 1)
    first = got_refs[0][0:PACK].astype(jnp.float32)[0:1]
    fill = jnp.where(lane < head_size, jnp.broadcast_to(first, (PACK, lanes)), 0.0)
    fill = fill.astype(jnp.bfloat16)
    blank = jnp.zeros((PACK, lanes), jnp.bfloat16)
    for start in range(0, size, PACK):
        kv_room[start : start + PACK] = fill
        live_room[start : start + PACK] = blank
    for start in range(0, query_ref.shape[0], PACK):
        query_ref[start : start + PACK] = blank
    left = lax.broadcasted_iota(jnp.int32, (half, lanes), 1) < head_size
    start = jnp.int32(0)
    for index, ref in enumerate(got_refs):
        for group, count in enumerate(source_counts(ref)):
            start_ref[MARKS * index + group] = start
            place = pl.ds(pl.multiple_of(start, PACK), rows)
            kv_room[place] = ref[group * rows : (group + 1) * rows]
            live = live_rows(count, rows, slot_rows, time_dev, lanes)
            live_room[place] = live.astype(jnp.float32).astype(jnp.bfloat16)
            base = 2 * rows + group * half
            pair = ref[base : base + half].astype(jnp.float32)
            query_ref[pl.ds(pl.multiple_of(start, PACK), half)] = jnp.where(left, pair, 0.0).astype(
                jnp.bfloat16
            )
            query_ref[pl.ds(pl.multiple_of(start + half, PACK), half)] = jnp.where(
                left, pltpu.roll(pair, head_size, 1), 0.0
            ).astype(jnp.bfloat16)
            start = start + packed_rows(count, slot_rows)
    start_ref[MARKS * len(got_refs)] = start
    case_ref[0] = jnp.clip((start - least + SIZE_STEP - 1) // SIZE_STEP, 0, cases - 1)


def pack(got, sizes, slot_rows, time_dev):
    message, lanes = got[0].shape
    rows = message // 3
    sources = MARKS * len(got)
    room = jax.ShapeDtypeStruct((sizes[-1] + rows, lanes), jnp.bfloat16)
    queries = up_to(sources * rows, QUERY_TILE) + rows
    return pl.pallas_call(
        functools.partial(pack_kernel, slot_rows, time_dev, sizes[0], len(sizes)),
        out_shape=(
            room,
            room,
            jax.ShapeDtypeStruct((queries, lanes), jnp.bfloat16),
            jax.ShapeDtypeStruct((sources + 1,), jnp.int32),
            jax.ShapeDtypeStruct((1,), jnp.int32),
        ),
        in_specs=[VMEM] * len(got),
        out_specs=(VMEM, VMEM, VMEM, SMEM, SMEM),
        compiler_params=params(),
        name="pack",
    )(*got)


def attend_kernel(first, last, lengths, *refs):
    start_ref, query_ref, live_ref = refs[:3]
    block_refs = refs[3 : 3 + len(lengths)]
    rest = list(refs[3 + len(lengths) :])
    side_ref = rest.pop()
    if not first:
        best_in, sum_in = rest[:2]
        rest = rest[2:]
    if last:
        sum_out = rest.pop()
        out_ref = rest[0]
    else:
        best_out, sum_out = rest
    lanes = live_ref.shape[1]
    head_size = lanes // 2
    blocks = []
    begin = 0
    for length, ref in zip(lengths, block_refs):
        left = lax.broadcasted_iota(jnp.int32, (length, lanes), 1) < head_size
        rows = slice(begin, begin + length)
        side_ref[rows] = jnp.where(left, live_ref[rows], ref[0:length])
        blocks.append((ref, length, rows))
        begin = begin + length
    total = start_ref[start_ref.shape[0] - 1]

    def chain(start, tile):
        place = pl.ds(pl.multiple_of(start, QUERY_TILE), tile)
        query = query_ref[place]
        scores = [
            lax.dot_general(
                query,
                ref[0:length],
                (((1,), (1,)), ((), ())),
                preferred_element_type=jnp.float32,
            )
            for ref, length, rows in blocks
        ]
        best = functools.reduce(
            jnp.maximum, [jnp.max(score, axis=-1, keepdims=True) for score in scores]
        )
        if not first:
            before = best_in[place][:, 0:1]
            best = jnp.maximum(best, before)
        sums = sum(
            jnp.dot(
                jnp.exp(score - best).astype(jnp.bfloat16),
                side_ref[rows],
                preferred_element_type=jnp.float32,
            )
            for score, (ref, length, rows) in zip(scores, blocks)
        )
        if not first:
            sums = sums + sum_in[place] * jnp.exp(before - best)
        if last:
            sums = sums / pltpu.roll(sums, head_size, 1)
        else:
            best_out[place] = jnp.broadcast_to(best, (tile, lanes))
        sum_out[place] = sums

    def step(index, carry):
        chain(index * QUERY_BIG, QUERY_BIG)
        return carry

    bigs = (total + QUERY_BIG - QUERY_TILE - 1) // QUERY_BIG
    lax.fori_loop(0, bigs, step, 0)

    @pl.when(total > bigs * QUERY_BIG)
    def _():
        chain(bigs * QUERY_BIG, QUERY_TILE)

    if last:
        half = out_ref.shape[1] // MARKS
        left_half = lax.broadcasted_iota(jnp.int32, (half, lanes), 1) < head_size
        for source in range(MARKS * out_ref.shape[0]):
            start = start_ref[source]
            top = sum_out[pl.ds(pl.multiple_of(start, PACK), half)]
            low = sum_out[pl.ds(pl.multiple_of(start + half, PACK), half)]
            base = source % MARKS * half
            out_ref[source // MARKS, base : base + half] = jnp.where(
                left_half, pltpu.roll(top, head_size, 1), low
            ).astype(jnp.bfloat16)


def run_stage(stage, stages, starts, query, live, blocks, lengths, state, half):
    lanes = query.shape[1]
    queries = query.shape[0]
    outs = (starts.shape[0] - 1) // MARKS
    first, last = stage == 0, stage == stages - 1
    held = jax.ShapeDtypeStruct((queries, lanes), jnp.float32)
    keys = sum(lengths)
    scratch = [pltpu.VMEM((keys, lanes), jnp.bfloat16)]
    if last:
        out_shape = (jax.ShapeDtypeStruct((outs, MARKS * half, lanes), jnp.bfloat16),)
        scratch = [pltpu.VMEM((queries, lanes), jnp.float32)] + scratch
    else:
        out_shape = (held, held)
    places = 3 + len(blocks)
    return pl.pallas_call(
        functools.partial(attend_kernel, first, last, lengths),
        out_shape=out_shape,
        in_specs=[SMEM] + [VMEM] * (2 + len(blocks) + len(state)),
        out_specs=(VMEM,) * len(out_shape),
        scratch_shapes=scratch,
        input_output_aliases={} if first or last else {places: 0, places + 1: 1},
        compiler_params=params(),
        cost_estimate=pl.CostEstimate(
            flops=4 * keys * keys * lanes, bytes_accessed=keys * lanes * 8, transcendentals=0
        ),
    )(starts, query, live, *blocks, *state)


def tie(value, *after):
    return lax.optimization_barrier((value, *after))


def attend_size(size, half, *packed):
    return exchange_and_attend(size, half, *packed)


def exchange_and_attend(size, half, kv, live, query, starts):
    late = up_to(size // 4, SIZE_STEP // 2)
    early = size - late
    first, second, both = tie(kv[:early], kv[early:size], kv[:size])
    far_early = lax.ppermute(first, "far", SWAP)
    far_late = lax.ppermute(second, "far", SWAP)
    near = lax.ppermute(both, "near", SWAP)
    run = lambda stage, blocks, lengths, state: run_stage(
        stage, 4, starts, query, live, blocks, lengths, state, half
    )
    state = run(0, (both,), (size,), ())
    near, *state = tie(near, *state)
    state = run(1, (near,), (size,), state)
    far_early, *state = tie(far_early, *state)
    both_early = lax.ppermute(far_early, "near", SWAP)
    both_late = lax.ppermute(far_late, "near", SWAP)
    state = run(2, (far_early, far_late), (early, late), state)
    both_early, both_late, *state = tie(both_early, both_late, *state)
    return run(3, (both_early, both_late), (early, late), state)[0]


def mix_kernel(core_ref, chip_ref, count_ref, got_ref, other_ref, x_ref, w_ref, out_ref, held_ref):
    chips, half, lanes = got_ref.shape
    time_dev, slots, width = x_ref.shape
    slot_rows = 2 * half // slots
    head_size = lanes // 2
    core = core_ref[0]
    chip = chip_ref[0]
    flipped = lax.rem(chip, 2) == 1
    left = lax.broadcasted_iota(jnp.int32, (half, lanes), 1) < head_size
    live = live_rows(count_ref[0], 2 * half, slot_rows, time_dev, lanes)
    for slot in range(chips // 2):
        block = (slot + chip // 2) % (chips // 2) if chips == 4 else slot
        for side in range(2):
            if side == 0:
                owner = core
                first = got_ref[2 * slot]
                second = got_ref[2 * slot + 1]
            else:
                owner = 1 - core
                first = other_ref[2 * slot]
                second = other_ref[2 * slot + 1]
            first = first.astype(jnp.float32)
            second = second.astype(jnp.float32)
            even = jnp.where(flipped, second, first)
            odd = jnp.where(flipped, first, second)
            top = jnp.where(left, even, pltpu.roll(odd, head_size, 1))
            low = jnp.where(left, pltpu.roll(even, head_size, 1), odd)
            pair = jnp.where(live, jnp.concatenate([top, low], axis=0), 0.0)
            place = pl.multiple_of((owner * (chips // 2) + block) * lanes, lanes)
            held_ref[:, pl.ds(place, lanes)] = pair.astype(jnp.bfloat16)
    hot = one_hot((time_dev * slots, 2 * half), slots, slot_rows, 1)
    attended = jnp.dot(hot, held_ref[...], preferred_element_type=jnp.float32).astype(jnp.bfloat16)
    mixed = jnp.dot(attended, w_ref[...], preferred_element_type=jnp.float32)
    full = x_ref[...].astype(jnp.float32) + mixed.reshape(time_dev, slots, width)
    slot = lax.broadcasted_iota(jnp.int32, full.shape, 1)
    out_ref[...] = jnp.where(slot < count_ref[0], full, 0.0).astype(jnp.bfloat16)


def mix(core, chip, count, got, other, tokens, w_out):
    half, _ = got.shape[1:]
    return pl.pallas_call(
        mix_kernel,
        out_shape=jax.ShapeDtypeStruct(tokens.shape, jnp.bfloat16),
        in_specs=[SMEM] * 3 + [VMEM] * 4,
        out_specs=VMEM,
        scratch_shapes=[pltpu.VMEM((2 * half, w_out.shape[0]), jnp.bfloat16)],
        compiler_params=params(),
        cost_estimate=pl.CostEstimate(
            flops=4 * half * w_out.size, bytes_accessed=2 * w_out.size, transcendentals=0
        ),
        name="mix",
    )(core, chip, count, got, other, tokens, w_out)


def spread(arrays, chips):
    return [arrays[0]] + [
        lax.ppermute(arrays[hop], "chip", [(i, i ^ hop) for i in range(chips)])
        for hop in range(1, chips)
    ]


def head_per_device(tokens, tube_count, ln_gain, ln_bias, w_qkv, w_out):
    slots, time_dev, _ = tokens.shape
    slot_rows = up_to(time_dev, SUBLANES)
    rows = slots * slot_rows
    half = rows // 2
    chips = lax.axis_size("chip")
    core = lax.axis_index("core").reshape(1)
    chip = lax.axis_index("chip").reshape(1)
    by_time = jnp.transpose(tokens, (1, 0, 2))
    other_tokens = lax.ppermute(by_time, "core", SWAP)
    other_count = lax.ppermute(tube_count, "core", SWAP)
    fetched = fetch(core, by_time, ln_gain, ln_bias, w_qkv, rows)
    rows_in, gain, bias, weights = fetched
    messages = project(
        chip, tube_count, other_count, rows_in, other_tokens, gain, bias, weights
    )
    got = spread(messages, chips)
    least = up_to((HEADS - 1) * up_to(slot_rows, PACK) + rows, SIZE_STEP) + SIZE_STEP
    most = up_to((HEADS - 1) * rows + up_to(slot_rows, PACK), SIZE_STEP)
    sizes = list(range(least, most, SIZE_STEP))[:SIZE_CASES] + [most]
    kv, live, query, starts, case = pack(got, sizes, slot_rows, time_dev)
    branches = [functools.partial(attend_size, size, half) for size in sizes]
    returned = lax.switch(case[0], branches, kv, live, query, starts)
    back = jnp.stack(spread(returned, chips))
    other = lax.ppermute(back[:, half:], "core", SWAP)
    mixed = mix(core, chip, tube_count, back[:, :half], other, by_time, w_out)
    return jnp.transpose(mixed, (1, 0, 2))


def layer_norm(flat, ln_gain, ln_bias):
    values32 = flat.astype(jnp.float32)
    center = values32 - jnp.mean(values32, axis=-1, keepdims=True)
    spread = jnp.mean(center * center, axis=-1, keepdims=True)
    return (center * lax.rsqrt(spread + EPSILON) * ln_gain + ln_bias).astype(jnp.bfloat16)


def live_mask(counts, slots_dev, time_dev):
    slot_ids = jnp.arange(slots_dev)[None, :, None]
    marks = jnp.broadcast_to(
        slot_ids < counts[:, None, None], (counts.shape[0], slots_dev, time_dev)
    )
    return marks.reshape(-1)


def attend(carry, query_heads, key_block, value_block, live_keys, scaling):
    best_now, total_now, accum = carry
    heads = query_heads.shape[1]
    key_heads = key_block.reshape(key_block.shape[0], heads, -1)
    value_heads = value_block.reshape(value_block.shape[0], heads, -1)
    scores = (
        jnp.einsum("qhd,khd->hqk", query_heads, key_heads, preferred_element_type=jnp.float32)
        * scaling
    )
    scores = jnp.where(live_keys[None, None, :], scores, NEG_FILL)
    best_next = jnp.maximum(best_now, jnp.max(scores, axis=-1))
    fading = jnp.exp(best_now - best_next)
    weights = jnp.exp(scores - best_next[..., None])
    total_next = total_now * fading + jnp.sum(weights, axis=-1)
    accum = accum * fading[..., None] + jnp.einsum(
        "hqk,khd->hqd",
        weights.astype(jnp.bfloat16),
        value_heads,
        preferred_element_type=jnp.float32,
    )
    return (best_next, total_next, accum)


def make_fold(query_heads, vis_dev, time_dev, scaling):
    rows_dev = vis_dev * time_dev

    def fold_masked(carry, piece, start):
        key_all, value_all, count_all = piece
        width_in = key_all.shape[1]
        shards = count_all.shape[0]
        group = 1
        for _ in range(6):
            if shards % (group * 2) == 0 and group * rows_dev < 2048:
                group = group * 2
        blocks = shards // group
        key_groups = key_all.reshape(blocks, group * rows_dev, width_in)
        value_groups = value_all.reshape(blocks, group * rows_dev, width_in)
        count_groups = count_all.reshape(blocks, group)

        def step_group(state, item):
            key_group, value_group, count_group = item
            marks = live_mask(count_group, vis_dev, time_dev)
            return (attend(state, query_heads, key_group, value_group, marks, scaling), None)

        carry, _ = lax.scan(step_group, carry, (key_groups, value_groups, count_groups))
        return carry

    return fold_masked


def start_state(heads, rows, head_size):
    return (
        jnp.full((heads, rows), NEG_FILL, jnp.float32),
        jnp.zeros((heads, rows), jnp.float32),
        jnp.zeros((heads, rows, head_size), jnp.float32),
    )


def on_device(tokens, tube_count, ln_gain, ln_bias, w_qkv, w_out):
    vis_dev, time_dev, width = tokens.shape
    rows_dev = vis_dev * time_dev
    inner = w_out.shape[0]
    head_size = inner // HEADS
    flat = tokens.reshape(rows_dev, width)
    normed = layer_norm(flat, ln_gain, ln_bias)
    projected = jnp.dot(normed, w_qkv, preferred_element_type=jnp.float32).astype(jnp.bfloat16)
    scaling = head_size ** (-0.5)
    frames = lax.axis_size("frame")
    local_heads = HEADS // frames
    stacked = projected.reshape(rows_dev, 3, HEADS, head_size)
    regrouped = lax.all_to_all(stacked, "frame", split_axis=2, concat_axis=0, tiled=True)
    all_rows = regrouped.shape[0]
    query_local = regrouped[:, 0]
    key_local = regrouped[:, 1].reshape(all_rows, local_heads * head_size)
    value_local = regrouped[:, 2].reshape(all_rows, local_heads * head_size)
    counts_rep = jnp.tile(tube_count, frames)
    fold_fn = make_fold(query_local, vis_dev, time_dev, scaling)
    state = fold_fn(
        start_state(local_heads, all_rows, head_size),
        (
            lax.all_gather(key_local, "space", axis=0, tiled=True),
            lax.all_gather(value_local, "space", axis=0, tiled=True),
            lax.all_gather(counts_rep, "space", axis=0, tiled=True),
        ),
        jnp.int32(0),
    )
    _, total_final, accum_final = state
    attended = (accum_final / total_final[..., None]).astype(jnp.bfloat16)
    attended = jnp.transpose(attended, (1, 0, 2))
    returned = lax.all_to_all(attended, "frame", split_axis=0, concat_axis=1, tiled=True)
    attended = returned.reshape(rows_dev, inner)
    mixed = flat.astype(jnp.float32) + jnp.dot(attended, w_out, preferred_element_type=jnp.float32)
    own_live = live_mask(tube_count, vis_dev, time_dev)
    mixed = jnp.where(own_live[:, None], mixed, 0.0)
    return mixed.astype(jnp.bfloat16).reshape(vis_dev, time_dev, width)


def solution(mesh):
    frames, spaces = mesh.shape["frame"], mesh.shape["space"]
    parts = (2, frames // 2, spaces // 2, 2)

    def layer(tokens, tube_count, ln_gain, ln_bias, w_qkv, w_out):
        slots = tokens.shape[0] // spaces
        time_dev = tokens.shape[1] // frames
        rows = slots * up_to(time_dev, SUBLANES)
        pairs = 2 * w_out.shape[0] == HEADS * LANES and rows % (2 * PACK) == 0
        padded = up_to(time_dev, SUBLANES) >= time_dev + MARKS
        split = parts[1] == 2 and parts[2] == 4 and spaces == HEADS
        if split and pairs and padded:
            run, over = head_per_device, Mesh(
                mesh.devices.reshape(parts), ("far", "near", "chip", "core")
            )
            frame, space = ("far", "near"), ("chip", "core")
        else:
            run, over, frame, space = on_device, mesh, "frame", "space"
        mapped = jax.shard_map(
            run,
            mesh=over,
            in_specs=(P(space, frame, None), P(space), P(), P(), P(), P()),
            out_specs=P(space, frame, None),
            check_vma=False,
        )
        return mapped(tokens, tube_count, ln_gain, ln_bias, w_qkv, w_out)

    return layer
```

profile of v0, /device:TPU:0, one launch (start us, length us, event | category | flops | bytes accessed | tf_op | source)
XLA Modules:
  0.0 55.9 jit_solution(599392680123482723)
XLA Ops:
  0.0 0.5 collective-permute-start.21
  0.5 0.0 collective-permute-start.20
  1.2 1.6 %fetch.1 = (bf16[160,1024]{1,0:T(8,128)(2,1)S(1)}, f32[1,1024]{1,0:T(1,128)S(1)}, f32[1,1024]{1,0:T(1,128)S(1)}, bf16[3,1024,256]{2,1,0:T(8,128)(2,1)S(1)}) custom-call(s32[1]{0:T(128)} %bitcast.core_ref, bf16[38,4,1024]{2,1,0:T(4,128)(2,1)} %bitcast.17, f32[1,1024]{1,0:T(1,128)} %bitcast.22, f32[1,1024]{1,0:T(1,128)} %bitcast.23, bf16[1024,1536]{1,0:T(8,128)(2,1)} %w_hbm.1), custom_call_target="tpu_custom_call" | custom-call | flops 503316480 | bytes 1572864 | tf_op jit(solution)/shard_map/fetch/pallas_call | solution.py:112
  2.7 2.0 %project.1 = (bf16[480,128]{1,0:T(8,128)(2,1)S(1)}, bf16[480,128]{1,0:T(8,128)(2,1)S(1)}, bf16[480,128]{1,0:T(8,128)(2,1)S(1)}, bf16[480,128]{1,0:T(8,128)(2,1)S(1)}) custom-call(s32[1]{0:T(128)} %bitcast.1.chip_ref, s32[1]{0:T(128)S(6)} %copy.43.count_ref, s32[1]{0:T(128)} %collective-permute-done.20.other_count_ref, ...), custom_call_target="tpu_custom_call" | custom-call | flops 503316480 | bytes 1572864 | tf_op jit(solution)/shard_map/project/pallas_call | solution.py:204
  4.7 3.0 %collective-permute-start.22 = (bf16[480,128]{1,0:T(8,128)(2,1)S(1)}, bf16[480,128]{1,0:T(8,128)(2,1)S(1)}, u32[]{:S(2)}, u32[]{:S(2)}) collective-permute-start(bf16[480,128]{1,0:T(8,128)(2,1)S(1)} %get-tuple-element.152), channel_id=1, source_target_pairs={{0,2},{2,0},{4,6},{6,4},{1,3},{3,1},{5,7},{7,5},{8,10},{10,8},{12,... | collective-permute-start | bytes 368648 | tf_op jit(solution)/shard_map/ppermute | solution.py:485
  7.8 1.5 %collective-permute-start.23 = (bf16[480,128]{1,0:T(8,128)(2,1)S(1)}, bf16[480,128]{1,0:T(8,128)(2,1)S(1)}, u32[]{:S(2)}, u32[]{:S(2)}) collective-permute-start(bf16[480,128]{1,0:T(8,128)(2,1)S(1)} %get-tuple-element.153), channel_id=1, source_target_pairs={{0,4},{2,6},{4,0},{6,2},{1,5},{3,7},{5,1},{7,3},{8,12},{10,14},{12... | collective-permute-start | bytes 368648 | tf_op jit(solution)/shard_map/ppermute | solution.py:485
  9.3 0.0 collective-permute-start.24
  9.3 2.2 %collective-permute-done.22.refs_1_ = bf16[480,128]{1,0:T(8,128)(2,1)S(1)} collective-permute-done((bf16[480,128]{1,0:T(8,128)(2,1)S(1)}, bf16[480,128]{1,0:T(8,128)(2,1)S(1)}, u32[]{:S(2)}, u32[]{:S(2)}) %collective-permute-start.22) | collective-permute-done | bytes 122912 | tf_op jit(solution)/shard_map/ppermute | solution.py:485
  11.5 3.9 %collective-permute-done.23.refs_2_ = bf16[480,128]{1,0:T(8,128)(2,1)S(1)} collective-permute-done((bf16[480,128]{1,0:T(8,128)(2,1)S(1)}, bf16[480,128]{1,0:T(8,128)(2,1)S(1)}, u32[]{:S(2)}, u32[]{:S(2)}) %collective-permute-start.23) | collective-permute-done | bytes 122912 | tf_op jit(solution)/shard_map/ppermute | solution.py:485
  15.4 0.9 %pack.1 = (bf16[1440,128]{1,0:T(8,128)(2,1)S(1)}, bf16[1440,128]{1,0:T(8,128)(2,1)S(1)}, bf16[1440,128]{1,0:T(8,128)(2,1)S(1)}, s32[9]{0:T(128)S(1)}, s32[1]{0:T(128)}) custom-call(bf16[480,128]{1,0:T(8,128)(2,1)S(1)} %get-tuple-element.151.refs_0_, bf16[480,128]{1,0:T(8,128)(2,1)S(1)} %collective-permute-done.22.refs_1_, ...), custom_call_target="tpu_custom_call" | custom-call | tf_op jit(solution)/shard_map/pack/pallas_call | solution.py:273
  16.9 0.0 copy-start
  17.0 30.3 %conditional.1 = (bf16[4,160,128]{2,1,0:T(8,128)(2,1)S(1)}) conditional(s32[]{:T(128)} %bitcast.5, (bf16[1440,128]{1,0:T(8,128)(2,1)S(1)}, s32[9]{0:T(128)S(1)}, bf16[1440,128]{1,0:T(8,128)(2,1)S(1)}, bf16[1440,128]{1,0:T(8,128)(2,1)S(1)}) %tuple.33, (bf16[1440,128]{1,0:T(8,128)(2,1)S(1)}, s32[9]{0:T(128)S(1)}, ...), branch_computations={%region_0.0_spmd, %region_1.0_spmd, %region_2.0_spmd, %region_3.0_... | conditional | flops 3355443200 | bytes 10485968 | solution.py:512
  17.3 1.6 %collective-permute-start.11 = (bf16[896,128]{1,0:T(8,128)(2,1)S(1)}, bf16[896,128]{1,0:T(8,128)(2,1)S(1)}, u32[]{:S(2)}, u32[]{:S(2)}) collective-permute-start(bf16[896,128]{1,0:T(8,128)(2,1)S(1)} %slice.44.refs_3_), channel_id=1, source_target_pairs={{0,8},{8,0},{1,9},{9,1},{2,10},{10,2},{3,11},{11,3},{4,12},{12,4},... | collective-permute-start | bytes 688136 | tf_op jit(solution)/shard_map/cond/branch_2_fun/ppermute | solution.py:414
  18.9 2.6 %collective-permute-start.10 = (bf16[640,128]{1,0:T(8,128)(2,1)S(1)}, bf16[640,128]{1,0:T(8,128)(2,1)S(1)}, u32[]{:S(2)}, u32[]{:S(2)}) collective-permute-start(bf16[640,128]{1,0:T(8,128)(2,1)S(1)} %slice.42), channel_id=1, source_target_pairs={{0,16},{16,0},{1,17},{17,1},{2,18},{18,2},{3,19},{19,3},{4,20},{20... | collective-permute-start | bytes 491528 | tf_op jit(solution)/shard_map/cond/branch_2_fun/ppermute | solution.py:412
  21.5 2.7 %branch_2_fun.4 = (f32[1440,128]{1,0:T(8,128)S(1)}, f32[1440,128]{1,0:T(8,128)S(1)}) custom-call(s32[9]{0:T(128)S(1)} %get-tuple-element.88.refs_0_, bf16[1440,128]{1,0:T(8,128)(2,1)S(1)} %get-tuple-element.89.refs_1_, bf16[1440,128]{1,0:T(8,128)(2,1)S(1)} %get-tuple-element.90.refs_2_, bf16[896,128]{1,0:T(8,128)(2,1)S(1)} %slice.44.refs_3_), custom_call_target="tpu_custom_call" | custom-call | flops 411041792 | bytes 917504 | tf_op jit(solution)/shard_map/cond/branch_2_fun/pallas_call | solution.py:386
  24.2 2.8 %collective-permute-done.11.refs_3_ = bf16[896,128]{1,0:T(8,128)(2,1)S(1)} collective-permute-done((bf16[896,128]{1,0:T(8,128)(2,1)S(1)}, bf16[896,128]{1,0:T(8,128)(2,1)S(1)}, u32[]{:S(2)}, u32[]{:S(2)}) %collective-permute-start.11) | collective-permute-done | bytes 229408 | tf_op jit(solution)/shard_map/cond/branch_2_fun/ppermute | solution.py:414
  27.0 3.7 %branch_2_fun.5 = (f32[1440,128]{1,0:T(8,128)S(1)}, f32[1440,128]{1,0:T(8,128)S(1)}) custom-call(s32[9]{0:T(128)S(1)} %get-tuple-element.88.refs_0_, bf16[1440,128]{1,0:T(8,128)(2,1)S(1)} %get-tuple-element.89.refs_1_, bf16[1440,128]{1,0:T(8,128)(2,1)S(1)} %get-tuple-element.90.refs_2_, ...), custom_call_target="tpu_custom_call", output_to_operand_aliasing={{0}: (4, {}), {1}: (5, {})} | custom-call | flops 411041792 | bytes 917504 | tf_op jit(solution)/shard_map/cond/branch_2_fun/pallas_call | solution.py:386
  30.7 0.1 collective-permute-start.12
  30.8 4.2 %collective-permute-start.13 = (bf16[256,128]{1,0:T(8,128)(2,1)S(1)}, bf16[256,128]{1,0:T(8,128)(2,1)S(1)}, u32[]{:S(2)}, u32[]{:S(2)}) collective-permute-start(bf16[256,128]{1,0:T(8,128)(2,1)S(1)} %slice.43), channel_id=1, source_target_pairs={{0,16},{16,0},{1,17},{17,1},{2,18},{18,2},{3,19},{19,3},{4,20},{20... | collective-permute-start | bytes 196616 | tf_op jit(solution)/shard_map/cond/branch_2_fun/ppermute | solution.py:413
  34.9 2.7 %collective-permute-done.13.refs_4_ = bf16[256,128]{1,0:T(8,128)(2,1)S(1)} collective-permute-done((bf16[256,128]{1,0:T(8,128)(2,1)S(1)}, bf16[256,128]{1,0:T(8,128)(2,1)S(1)}, u32[]{:S(2)}, u32[]{:S(2)}) %collective-permute-start.13) | collective-permute-done | bytes 65568 | tf_op jit(solution)/shard_map/cond/branch_2_fun/ppermute | solution.py:413
  37.6 2.0 %collective-permute-start.14 = (bf16[256,128]{1,0:T(8,128)(2,1)S(1)}, bf16[256,128]{1,0:T(8,128)(2,1)S(1)}, u32[]{:S(2)}, u32[]{:S(2)}) collective-permute-start(bf16[256,128]{1,0:T(8,128)(2,1)S(1)} %collective-permute-done.13.refs_4_), channel_id=1, source_target_pairs={{0,8},{8,0},{1,9},{9,1},{2,10},{10,2},{3,11},{11,3},{4,12},{12,4},... | collective-permute-start | bytes 196616 | tf_op jit(solution)/shard_map/cond/branch_2_fun/ppermute | solution.py:423
  39.6 3.5 %branch_2_fun.6 = (f32[1440,128]{1,0:T(8,128)S(1)}, f32[1440,128]{1,0:T(8,128)S(1)}) custom-call(s32[9]{0:T(128)S(1)} %get-tuple-element.88.refs_0_, bf16[1440,128]{1,0:T(8,128)(2,1)S(1)} %get-tuple-element.89.refs_1_, bf16[1440,128]{1,0:T(8,128)(2,1)S(1)} %get-tuple-element.90.refs_2_, ...), custom_call_target="tpu_custom_call", output_to_operand_aliasing={{0}: (5, {}), {1}: (6, {})} | custom-call | flops 411041792 | bytes 917504 | tf_op jit(solution)/shard_map/cond/branch_2_fun/pallas_call | solution.py:386
  43.2 3.8 %branch_2_fun.7 = bf16[4,160,128]{2,1,0:T(8,128)(2,1)S(1)} custom-call(s32[9]{0:T(128)S(1)} %get-tuple-element.88.refs_0_, bf16[1440,128]{1,0:T(8,128)(2,1)S(1)} %get-tuple-element.89.refs_1_, bf16[1440,128]{1,0:T(8,128)(2,1)S(1)} %get-tuple-element.90.refs_2_, bf16[640,128]{1,0:T(8,128)(2,1)S(1)} %collective-permute-done.12.refs_3_, ...), custom_call_target="tpu_custom_call" | custom-call | flops 411041792 | bytes 917504 | tf_op jit(solution)/shard_map/cond/branch_2_fun/pallas_call | solution.py:386
  47.2 1.7 %collective-permute-start.27 = (bf16[160,128]{1,0:T(8,128)(2,1)S(1)}, bf16[160,128]{1,0:T(8,128)(2,1)S(1)}, u32[]{:S(2)}, u32[]{:S(2)}) collective-permute-start(bf16[160,128]{1,0:T(8,128)(2,1)S(1)} %get-tuple-element.163), channel_id=1, source_target_pairs={{0,6},{2,4},{4,2},{6,0},{1,7},{3,5},{5,3},{7,1},{8,14},{10,12},{12... | collective-permute-start | bytes 122888 | tf_op jit(solution)/shard_map/ppermute | solution.py:485
  49.0 0.1 collective-permute-start.25
  49.1 1.7 %collective-permute-start.26 = (bf16[160,128]{1,0:T(8,128)(2,1)S(1)}, bf16[160,128]{1,0:T(8,128)(2,1)S(1)}, u32[]{:S(2)}, u32[]{:S(2)}) collective-permute-start(bf16[160,128]{1,0:T(8,128)(2,1)S(1)} %get-tuple-element.164), channel_id=1, source_target_pairs={{0,4},{2,6},{4,0},{6,2},{1,5},{3,7},{5,1},{7,3},{8,12},{10,14},{12... | collective-permute-start | bytes 122888 | tf_op jit(solution)/shard_map/ppermute | solution.py:485
  50.8 1.4 %collective-permute-done.27 = bf16[160,128]{1,0:T(8,128)(2,1)S(1)} collective-permute-done((bf16[160,128]{1,0:T(8,128)(2,1)S(1)}, bf16[160,128]{1,0:T(8,128)(2,1)S(1)}, u32[]{:S(2)}, u32[]{:S(2)}) %collective-permute-start.27) | collective-permute-done | bytes 40992 | tf_op jit(solution)/shard_map/ppermute | solution.py:485
  52.2 0.8 %collective-permute-done.25 = bf16[160,128]{1,0:T(8,128)(2,1)S(1)} collective-permute-done((bf16[160,128]{1,0:T(8,128)(2,1)S(1)}, bf16[160,128]{1,0:T(8,128)(2,1)S(1)}, u32[]{:S(2)}, u32[]{:S(2)}) %collective-permute-start.25) | collective-permute-done | bytes 40992 | tf_op jit(solution)/shard_map/ppermute | solution.py:485
  53.0 0.1 collective-permute-done.26
  53.2 0.1 collective-permute-start.28
  53.2 1.3 %collective-permute-done.28.other_ref = bf16[4,80,128]{2,1,0:T(8,128)(2,1)S(1)} collective-permute-done((bf16[4,80,128]{2,1,0:T(8,128)(2,1)S(1)}, bf16[4,80,128]{2,1,0:T(8,128)(2,1)S(1)}, u32[]{:S(2)}, u32[]{:S(2)}) %collective-permute-start.28) | collective-permute-done | bytes 81952 | tf_op jit(solution)/shard_map/ppermute | solution.py:514
  54.5 1.3 %mix.1 = bf16[38,4,1024]{2,1,0:T(4,128)(2,1)} custom-call(s32[1]{0:T(128)} %bitcast.core_ref, s32[1]{0:T(128)} %bitcast.1.chip_ref, s32[1]{0:T(128)S(6)} %copy.43.count_ref, bf16[4,80,128]{2,1,0:T(8,128)(2,1)S(1)} %get-tuple-element.161.got_ref, bf16[4,80,128]{2,1,0:T(8,128)(2,1)S(1)} %collective-permute-done.28.other_ref, ...), custom_call_target="tpu_custom_call" | custom-call | flops 167772160 | bytes 1048576 | tf_op jit(solution)/shard_map/mix/pallas_call | solution.py:469
  (15 shorter events, 0.1 us)
Async XLA Ops:
  0.0 2.7 %collective-permute-start.21 = (bf16[38,4,1024]{2,1,0:T(4,128)(2,1)}, bf16[38,4,1024]{2,1,0:T(4,128)(2,1)S(1)}, u32[]{:S(2)}, u32[]{:S(2)}) collective-permute-start(bf16[38,4,1024]{2,1,0:T(4,128)(2,1)} %bitcast.16), channel_id=1, source_target_pairs={{0,1},{1,0},{2,3},{3,2},{4,5},{5,4},{6,7},{7,6},{8,9},{9,8},{10,11... | collective-permute-start | bytes 933896 | tf_op jit(solution)/shard_map/ppermute | solution.py:499
  0.5 2.2 %collective-permute-start.20 = (s32[1]{0:T(128)}, s32[1]{0:T(128)}, u32[]{:S(2)}, u32[]{:S(2)}) collective-permute-start(s32[1]{0:T(128)} %param.11), channel_id=1, source_target_pairs={{0,1},{1,0},{2,3},{3,2},{4,5},{5,4},{6,7},{7,6},{8,9},{9,8},{10,11... | collective-permute-start | bytes 20 | tf_op jit(solution)/shard_map/ppermute | solution.py:500
  4.7 6.7 %collective-permute-start.22 = (bf16[480,128]{1,0:T(8,128)(2,1)S(1)}, bf16[480,128]{1,0:T(8,128)(2,1)S(1)}, u32[]{:S(2)}, u32[]{:S(2)}) collective-permute-start(bf16[480,128]{1,0:T(8,128)(2,1)S(1)} %get-tuple-element.152), channel_id=1, source_target_pairs={{0,2},{2,0},{4,6},{6,4},{1,3},{3,1},{5,7},{7,5},{8,10},{10,8},{12,... | collective-permute-start | bytes 368648 | tf_op jit(solution)/shard_map/ppermute | solution.py:485
  7.8 7.6 %collective-permute-start.23 = (bf16[480,128]{1,0:T(8,128)(2,1)S(1)}, bf16[480,128]{1,0:T(8,128)(2,1)S(1)}, u32[]{:S(2)}, u32[]{:S(2)}) collective-permute-start(bf16[480,128]{1,0:T(8,128)(2,1)S(1)} %get-tuple-element.153), channel_id=1, source_target_pairs={{0,4},{2,6},{4,0},{6,2},{1,5},{3,7},{5,1},{7,3},{8,12},{10,14},{12... | collective-permute-start | bytes 368648 | tf_op jit(solution)/shard_map/ppermute | solution.py:485
  9.3 6.1 %collective-permute-start.24 = (bf16[480,128]{1,0:T(8,128)(2,1)S(1)}, bf16[480,128]{1,0:T(8,128)(2,1)S(1)}, u32[]{:S(2)}, u32[]{:S(2)}) collective-permute-start(bf16[480,128]{1,0:T(8,128)(2,1)S(1)} %get-tuple-element.154), channel_id=1, source_target_pairs={{0,6},{2,4},{4,2},{6,0},{1,7},{3,5},{5,3},{7,1},{8,14},{10,12},{12... | collective-permute-start | bytes 368648 | tf_op jit(solution)/shard_map/ppermute | solution.py:485
  16.9 37.6 %copy-start = (bf16[4,38,1024]{2,0,1:T(4,128)(2,1)S(1)}, bf16[4,38,1024]{2,0,1:T(4,128)(2,1)}, u32[]{:S(2)}) copy-start(bf16[4,38,1024]{2,0,1:T(4,128)(2,1)} %param.10) | copy-start | bytes 933892
  16.9 37.6 %copy-start.1 = (bf16[512,1024]{1,0:T(8,128)(2,1)S(1)}, bf16[512,1024]{1,0:T(8,128)(2,1)}, u32[]{:S(2)}) copy-start(bf16[512,1024]{1,0:T(8,128)(2,1)} %w_ref.1) | copy-start | bytes 3145732
  17.3 9.7 %collective-permute-start.11 = (bf16[896,128]{1,0:T(8,128)(2,1)S(1)}, bf16[896,128]{1,0:T(8,128)(2,1)S(1)}, u32[]{:S(2)}, u32[]{:S(2)}) collective-permute-start(bf16[896,128]{1,0:T(8,128)(2,1)S(1)} %slice.44.refs_3_), channel_id=1, source_target_pairs={{0,8},{8,0},{1,9},{9,1},{2,10},{10,2},{3,11},{11,3},{4,12},{12,4},... | collective-permute-start | bytes 688136 | tf_op jit(solution)/shard_map/cond/branch_2_fun/ppermute | solution.py:414
  18.9 11.8 %collective-permute-start.10 = (bf16[640,128]{1,0:T(8,128)(2,1)S(1)}, bf16[640,128]{1,0:T(8,128)(2,1)S(1)}, u32[]{:S(2)}, u32[]{:S(2)}) collective-permute-start(bf16[640,128]{1,0:T(8,128)(2,1)S(1)} %slice.42), channel_id=1, source_target_pairs={{0,16},{16,0},{1,17},{17,1},{2,18},{18,2},{3,19},{19,3},{4,20},{20... | collective-permute-start | bytes 491528 | tf_op jit(solution)/shard_map/cond/branch_2_fun/ppermute | solution.py:412
  30.7 12.5 %collective-permute-start.12 = (bf16[640,128]{1,0:T(8,128)(2,1)S(1)}, bf16[640,128]{1,0:T(8,128)(2,1)S(1)}, u32[]{:S(2)}, u32[]{:S(2)}) collective-permute-start(bf16[640,128]{1,0:T(8,128)(2,1)S(1)} %collective-permute-done.10.refs_3_), channel_id=1, source_target_pairs={{0,8},{8,0},{1,9},{9,1},{2,10},{10,2},{3,11},{11,3},{4,12},{12,4},... | collective-permute-start | bytes 491528 | tf_op jit(solution)/shard_map/cond/branch_2_fun/ppermute | solution.py:422
  30.8 6.8 %collective-permute-start.13 = (bf16[256,128]{1,0:T(8,128)(2,1)S(1)}, bf16[256,128]{1,0:T(8,128)(2,1)S(1)}, u32[]{:S(2)}, u32[]{:S(2)}) collective-permute-start(bf16[256,128]{1,0:T(8,128)(2,1)S(1)} %slice.43), channel_id=1, source_target_pairs={{0,16},{16,0},{1,17},{17,1},{2,18},{18,2},{3,19},{19,3},{4,20},{20... | collective-permute-start | bytes 196616 | tf_op jit(solution)/shard_map/cond/branch_2_fun/ppermute | solution.py:413
  37.6 5.5 %collective-permute-start.14 = (bf16[256,128]{1,0:T(8,128)(2,1)S(1)}, bf16[256,128]{1,0:T(8,128)(2,1)S(1)}, u32[]{:S(2)}, u32[]{:S(2)}) collective-permute-start(bf16[256,128]{1,0:T(8,128)(2,1)S(1)} %collective-permute-done.13.refs_4_), channel_id=1, source_target_pairs={{0,8},{8,0},{1,9},{9,1},{2,10},{10,2},{3,11},{11,3},{4,12},{12,4},... | collective-permute-start | bytes 196616 | tf_op jit(solution)/shard_map/cond/branch_2_fun/ppermute | solution.py:423
  47.2 5.0 %collective-permute-start.27 = (bf16[160,128]{1,0:T(8,128)(2,1)S(1)}, bf16[160,128]{1,0:T(8,128)(2,1)S(1)}, u32[]{:S(2)}, u32[]{:S(2)}) collective-permute-start(bf16[160,128]{1,0:T(8,128)(2,1)S(1)} %get-tuple-element.163), channel_id=1, source_target_pairs={{0,6},{2,4},{4,2},{6,0},{1,7},{3,5},{5,3},{7,1},{8,14},{10,12},{12... | collective-permute-start | bytes 122888 | tf_op jit(solution)/shard_map/ppermute | solution.py:485
  49.0 4.0 %collective-permute-start.25 = (bf16[160,128]{1,0:T(8,128)(2,1)S(1)}, bf16[160,128]{1,0:T(8,128)(2,1)S(1)}, u32[]{:S(2)}, u32[]{:S(2)}) collective-permute-start(bf16[160,128]{1,0:T(8,128)(2,1)S(1)} %get-tuple-element.165), channel_id=1, source_target_pairs={{0,2},{2,0},{4,6},{6,4},{1,3},{3,1},{5,7},{7,5},{8,10},{10,8},{12,... | collective-permute-start | bytes 122888 | tf_op jit(solution)/shard_map/ppermute | solution.py:485
  49.1 4.0 %collective-permute-start.26 = (bf16[160,128]{1,0:T(8,128)(2,1)S(1)}, bf16[160,128]{1,0:T(8,128)(2,1)S(1)}, u32[]{:S(2)}, u32[]{:S(2)}) collective-permute-start(bf16[160,128]{1,0:T(8,128)(2,1)S(1)} %get-tuple-element.164), channel_id=1, source_target_pairs={{0,4},{2,6},{4,0},{6,2},{1,5},{3,7},{5,1},{7,3},{8,12},{10,14},{12... | collective-permute-start | bytes 122888 | tf_op jit(solution)/shard_map/ppermute | solution.py:485
  53.2 1.3 %collective-permute-start.28 = (bf16[4,80,128]{2,1,0:T(8,128)(2,1)S(1)}, bf16[4,80,128]{2,1,0:T(8,128)(2,1)S(1)}, u32[]{:S(2)}, u32[]{:S(2)}) collective-permute-start(bf16[4,80,128]{2,1,0:T(8,128)(2,1)S(1)} %get-tuple-element.160), channel_id=1, source_target_pairs={{0,1},{1,0},{2,3},{3,2},{4,5},{5,4},{6,7},{7,6},{8,9},{9,8},{10,11... | collective-permute-start | bytes 245768 | tf_op jit(solution)/shard_map/ppermute | solution.py:514
where the time goes:
time: 56 us; the launch traced here: 55.9 us
  Pallas kernels  19.4 us (35%)
  starting transfers between devices  19.2 us (34%)
  waiting for transfers between devices  15.1 us (27%)
  between operations  1.4 us (2%)
  loops' own time  0.64 us (1%)
    pallas_call x4, Pallas kernels, run_stage(): pl.pallas_call(functools.partial(attend_kernel, first, last, lengths), ou...  13.6 us
    ppermute x6, waiting for transfers between devices, spread(): lax.ppermute(arrays[hop], 'chip', [(i, i ^ hop) for i in range(chips)])  8.36 us
    ppermute x6, starting transfers between devices, spread(): lax.ppermute(arrays[hop], 'chip', [(i, i ^ hop) for i in range(chips)])  8.12 us
    ppermute x1, starting transfers between devices, exchange_and_attend(): far_late = lax.ppermute(second, 'far', SWAP)  4.15 us
    ppermute x1, waiting for transfers between devices, exchange_and_attend(): near = lax.ppermute(both, 'near', SWAP)  2.76 us
    ppermute x1, waiting for transfers between devices, exchange_and_attend(): far_late = lax.ppermute(second, 'far', SWAP)  2.67 us
    ppermute x1, starting transfers between devices, exchange_and_attend(): far_early = lax.ppermute(first, 'far', SWAP)  2.59 us
    ppermute x1, starting transfers between devices, exchange_and_attend(): both_late = lax.ppermute(far_late, 'near', SWAP)  2.04 us
  transfers between devices with their start and end apart: 14, of which 8 were waited for; matrix products, arithmetic and copies ran while one was open for 0% of the time, Pallas kernels for 20%

commit v1 on v0

--- a/solution.py
+++ b/solution.py
@@ -15,8 +15,10 @@
 SUBLANES = 8
 PACK = 16
 SIZE_STEP = 128
-SIZE_CASES = 3
 MARKS = 2
+SIZES_ABOVE = (128, 192, 320, 448)
+SCORE_BOUND = 60.0
+QUERY_SMALL = 128
 QUERY_TILE = 256
 QUERY_BIG = 512
 VMEM_BYTES = 20 * 2**20
@@ -35,7 +37,7 @@
 
 
 def packed_rows(count, slot_rows):
-    return (count * slot_rows + PACK - 1) // PACK * PACK
+    return count * slot_rows
 
 
 def slot_of(row, slots, slot_rows):
@@ -57,6 +59,10 @@
     slot = slot_of(padded, slots, slot_rows)
     hot = plain == (padded - slot * slot_rows) * slots + slot
     return hot.astype(jnp.float32).astype(jnp.bfloat16)
+
+
+def scalar(ref):
+    return jnp.max(ref[...].astype(jnp.float32)).astype(jnp.int32)
 
 
 def normalise(x_ref, gain_ref, bias_ref, rows):
@@ -161,7 +167,7 @@
     left = lax.broadcasted_iota(jnp.int32, (rows, lanes), 1) < head_size
     left_half = left[:half]
     row_half = lax.broadcasted_iota(jnp.int32, (half, lanes), 0)
-    counts = (count_ref[0], other_count_ref[0])
+    counts = (scalar(count_ref), scalar(other_count_ref))
     flipped = lax.rem(chip, 2) == 1
     for slot in range(chips // 2):
         block = (slot + chip // 2) % (chips // 2) if chips == 4 else slot
@@ -204,7 +210,7 @@
     return pl.pallas_call(
         project_kernel,
         out_shape=(message,) * chips,
-        in_specs=[SMEM] * 3 + [VMEM] * 5,
+        in_specs=[SMEM] + [VMEM] * 7,
         out_specs=(VMEM,) * chips,
         scratch_shapes=[held] * 3,
         compiler_params=params(),
@@ -224,7 +230,7 @@
     ]
 
 
-def pack_kernel(slot_rows, time_dev, least, cases, *refs):
+def pack_kernel(slot_rows, time_dev, sizes, *refs):
     got_refs = refs[:-5]
     kv_room, live_room, query_ref, start_ref, case_ref = refs[-5:]
     message, lanes = got_refs[0].shape
@@ -243,25 +249,26 @@
     for start in range(0, query_ref.shape[0], PACK):
         query_ref[start : start + PACK] = blank
     left = lax.broadcasted_iota(jnp.int32, (half, lanes), 1) < head_size
+    plain = left & (lax.broadcasted_iota(jnp.int32, (half, lanes), 0) < half - MARKS)
     start = jnp.int32(0)
     for index, ref in enumerate(got_refs):
         for group, count in enumerate(source_counts(ref)):
             start_ref[MARKS * index + group] = start
-            place = pl.ds(pl.multiple_of(start, PACK), rows)
+            place = pl.ds(pl.multiple_of(start, SUBLANES), rows)
             kv_room[place] = ref[group * rows : (group + 1) * rows]
             live = live_rows(count, rows, slot_rows, time_dev, lanes)
             live_room[place] = live.astype(jnp.float32).astype(jnp.bfloat16)
             base = 2 * rows + group * half
             pair = ref[base : base + half].astype(jnp.float32)
-            query_ref[pl.ds(pl.multiple_of(start, PACK), half)] = jnp.where(left, pair, 0.0).astype(
+            query_ref[pl.ds(pl.multiple_of(start, SUBLANES), half)] = jnp.where(left, pair, 0.0).astype(
                 jnp.bfloat16
             )
-            query_ref[pl.ds(pl.multiple_of(start + half, PACK), half)] = jnp.where(
-                left, pltpu.roll(pair, head_size, 1), 0.0
+            query_ref[pl.ds(pl.multiple_of(start + half, SUBLANES), half)] = jnp.where(
+                plain, pltpu.roll(pair, head_size, 1), 0.0
             ).astype(jnp.bfloat16)
             start = start + packed_rows(count, slot_rows)
     start_ref[MARKS * len(got_refs)] = start
-    case_ref[0] = jnp.clip((start - least + SIZE_STEP - 1) // SIZE_STEP, 0, cases - 1)
+    case_ref[0] = sum((start > size).astype(jnp.int32) for size in sizes[:-1])
 
 
 def pack(got, sizes, slot_rows, time_dev):
@@ -271,7 +278,7 @@
     room = jax.ShapeDtypeStruct((sizes[-1] + rows, lanes), jnp.bfloat16)
     queries = up_to(sources * rows, QUERY_TILE) + rows
     return pl.pallas_call(
-        functools.partial(pack_kernel, slot_rows, time_dev, sizes[0], len(sizes)),
+        functools.partial(pack_kernel, slot_rows, time_dev, tuple(sizes)),
         out_shape=(
             room,
             room,
@@ -286,108 +293,153 @@
     )(*got)
 
 
-def attend_kernel(first, last, lengths, *refs):
+def attend_kernel(first, last, size, lengths, *refs):
     start_ref, query_ref, live_ref = refs[:3]
     block_refs = refs[3 : 3 + len(lengths)]
     rest = list(refs[3 + len(lengths) :])
     side_ref = rest.pop()
     if not first:
-        best_in, sum_in = rest[:2]
-        rest = rest[2:]
+        best_in, sum_in, flag_in = rest[:3]
+        rest = rest[3:]
     if last:
         sum_out = rest.pop()
         out_ref = rest[0]
     else:
-        best_out, sum_out = rest
+        best_out, sum_out, flag_out = rest
     lanes = live_ref.shape[1]
     head_size = lanes // 2
+    total = start_ref[start_ref.shape[0] - 1]
     blocks = []
     begin = 0
+    widest = jnp.zeros((1, lanes), jnp.float32)
     for length, ref in zip(lengths, block_refs):
         left = lax.broadcasted_iota(jnp.int32, (length, lanes), 1) < head_size
         rows = slice(begin, begin + length)
-        side_ref[rows] = jnp.where(left, live_ref[rows], ref[0:length])
+        place = begin % size
+        side_ref[rows] = jnp.where(left, live_ref[place : place + length], ref[0:length])
+        reach = jnp.max(jnp.abs(ref[0:length].astype(jnp.float32)), axis=0, keepdims=True)
+        widest = jnp.maximum(widest, reach)
         blocks.append((ref, length, rows))
         begin = begin + length
-    total = start_ref[start_ref.shape[0] - 1]
-
-    def chain(start, tile):
+    lane = lax.broadcasted_iota(jnp.int32, (1, lanes), 1)
+    keys_square = jnp.sum(jnp.where(lane < head_size, widest * widest, 0.0))
+    if first:
+        queries = query_ref[0 : query_ref.shape[0] // QUERY_TILE * QUERY_TILE].astype(jnp.float32)
+        query_square = jnp.max(jnp.sum(queries * queries, axis=-1, keepdims=True))
+        small = jnp.bool_(True)
+    else:
+        query_square = flag_in[0]
+        small = flag_in[1] > 0.5
+    before_small = small
+    small = jnp.logical_and(small, query_square * keys_square <= SCORE_BOUND * SCORE_BOUND)
+    if not last:
+        flag_out[0] = query_square
+        flag_out[1] = jnp.where(small, 1.0, 0.0)
+
+    def score(query, ref, length):
+        return lax.dot_general(
+            query, ref[0:length], (((1,), (1,)), ((), ())), preferred_element_type=jnp.float32
+        )
+
+    def total_of(weights):
+        return sum(
+            jnp.dot(weight, side_ref[rows], preferred_element_type=jnp.float32)
+            for weight, (ref, length, rows) in zip(weights, blocks)
+        )
+
+    def finish(place, sums):
+        if last:
+            sums = sums / pltpu.roll(sums, head_size, 1)
+        sum_out[place] = sums
+
+    def unshifted(start, tile):
         place = pl.ds(pl.multiple_of(start, QUERY_TILE), tile)
         query = query_ref[place]
-        scores = [
-            lax.dot_general(
-                query,
-                ref[0:length],
-                (((1,), (1,)), ((), ())),
-                preferred_element_type=jnp.float32,
-            )
-            for ref, length, rows in blocks
-        ]
-        best = functools.reduce(
-            jnp.maximum, [jnp.max(score, axis=-1, keepdims=True) for score in scores]
+        sums = total_of(
+            [
+                jnp.exp(score(query, ref, length)).astype(jnp.bfloat16)
+                for ref, length, rows in blocks
+            ]
         )
         if not first:
-            before = best_in[place][:, 0:1]
-            best = jnp.maximum(best, before)
-        sums = sum(
-            jnp.dot(
-                jnp.exp(score - best).astype(jnp.bfloat16),
-                side_ref[rows],
-                preferred_element_type=jnp.float32,
-            )
-            for score, (ref, length, rows) in zip(scores, blocks)
+            sums = sums + sum_in[place]
+        finish(place, sums)
+
+    def shifted(start, tile):
+        place = pl.ds(pl.multiple_of(start, tile), tile)
+        query = query_ref[place]
+        scores = [score(query, ref, length) for ref, length, rows in blocks]
+        best = functools.reduce(
+            jnp.maximum, [jnp.max(part, axis=-1, keepdims=True) for part in scores]
         )
         if not first:
+            before = jnp.where(before_small, 0.0, best_in[place][:, 0:1])
+            best = jnp.maximum(best, before)
+        sums = total_of([jnp.exp(part - best).astype(jnp.bfloat16) for part in scores])
+        if not first:
             sums = sums + sum_in[place] * jnp.exp(before - best)
-        if last:
-            sums = sums / pltpu.roll(sums, head_size, 1)
-        else:
+        if not last:
             best_out[place] = jnp.broadcast_to(best, (tile, lanes))
-        sum_out[place] = sums
-
-    def step(index, carry):
-        chain(index * QUERY_BIG, QUERY_BIG)
-        return carry
-
-    bigs = (total + QUERY_BIG - QUERY_TILE - 1) // QUERY_BIG
-    lax.fori_loop(0, bigs, step, 0)
-
-    @pl.when(total > bigs * QUERY_BIG)
+        finish(place, sums)
+
+    @pl.when(small)
     def _():
-        chain(bigs * QUERY_BIG, QUERY_TILE)
+        def step(index, carry):
+            unshifted(index * QUERY_BIG, QUERY_BIG)
+            return carry
+
+        bigs = (total + QUERY_BIG - QUERY_TILE - 1) // QUERY_BIG
+        lax.fori_loop(0, bigs, step, 0)
+
+        @pl.when(total > bigs * QUERY_BIG)
+        def _():
+            unshifted(bigs * QUERY_BIG, QUERY_TILE)
+
+    @pl.when(jnp.logical_not(small))
+    def _():
+        def step(index, carry):
+            shifted(index * QUERY_SMALL, QUERY_SMALL)
+            return carry
+
+        lax.fori_loop(0, (total + QUERY_SMALL - 1) // QUERY_SMALL, step, 0)
 
     if last:
         half = out_ref.shape[1] // MARKS
         left_half = lax.broadcasted_iota(jnp.int32, (half, lanes), 1) < head_size
         for source in range(MARKS * out_ref.shape[0]):
             start = start_ref[source]
-            top = sum_out[pl.ds(pl.multiple_of(start, PACK), half)]
-            low = sum_out[pl.ds(pl.multiple_of(start + half, PACK), half)]
+            top = sum_out[pl.ds(pl.multiple_of(start, SUBLANES), half)]
+            low = sum_out[pl.ds(pl.multiple_of(start + half, SUBLANES), half)]
             base = source % MARKS * half
             out_ref[source // MARKS, base : base + half] = jnp.where(
                 left_half, pltpu.roll(top, head_size, 1), low
             ).astype(jnp.bfloat16)
 
 
-def run_stage(stage, stages, starts, query, live, blocks, lengths, state, half):
+def run_stage(stage, stages, size, starts, query, live, blocks, lengths, state, half):
     lanes = query.shape[1]
     queries = query.shape[0]
     outs = (starts.shape[0] - 1) // MARKS
     first, last = stage == 0, stage == stages - 1
     held = jax.ShapeDtypeStruct((queries, lanes), jnp.float32)
+    flags = jax.ShapeDtypeStruct((2,), jnp.float32)
     keys = sum(lengths)
     scratch = [pltpu.VMEM((keys, lanes), jnp.bfloat16)]
     if last:
         out_shape = (jax.ShapeDtypeStruct((outs, MARKS * half, lanes), jnp.bfloat16),)
+        out_specs = (VMEM,)
         scratch = [pltpu.VMEM((queries, lanes), jnp.float32)] + scratch
     else:
-        out_shape = (held, held)
+        out_shape = (held, held, flags)
+        out_specs = (VMEM, VMEM, SMEM)
     places = 3 + len(blocks)
     return pl.pallas_call(
-        functools.partial(attend_kernel, first, last, lengths),
+        functools.partial(attend_kernel, first, last, size, lengths),
         out_shape=out_shape,
-        in_specs=[SMEM] + [VMEM] * (2 + len(blocks) + len(state)),
-        out_specs=(VMEM,) * len(out_shape),
+        in_specs=[SMEM]
+        + [VMEM] * (2 + len(blocks))
+        + ([] if first else [VMEM, VMEM, SMEM]),
+        out_specs=out_specs,
         scratch_shapes=scratch,
         input_output_aliases={} if first or last else {places: 0, places + 1: 1},
         compiler_params=params(),
@@ -406,24 +458,22 @@
 
 
 def exchange_and_attend(size, half, kv, live, query, starts):
-    late = up_to(size // 4, SIZE_STEP // 2)
+    late = size // 2 // SIZE_STEP * SIZE_STEP
     early = size - late
     first, second, both = tie(kv[:early], kv[early:size], kv[:size])
     far_early = lax.ppermute(first, "far", SWAP)
     far_late = lax.ppermute(second, "far", SWAP)
     near = lax.ppermute(both, "near", SWAP)
     run = lambda stage, blocks, lengths, state: run_stage(
-        stage, 4, starts, query, live, blocks, lengths, state, half
+        stage, 3, size, starts, query, live, blocks, lengths, state, half
     )
     state = run(0, (both,), (size,), ())
-    near, *state = tie(near, *state)
-    state = run(1, (near,), (size,), state)
     far_early, *state = tie(far_early, *state)
     both_early = lax.ppermute(far_early, "near", SWAP)
     both_late = lax.ppermute(far_late, "near", SWAP)
-    state = run(2, (far_early, far_late), (early, late), state)
+    state = run(1, (near, far_early, far_late), (size, early, late), state)
     both_early, both_late, *state = tie(both_early, both_late, *state)
-    return run(3, (both_early, both_late), (early, late), state)[0]
+    return run(2, (both_early, both_late), (early, late), state)[0]
 
 
 def mix_kernel(core_ref, chip_ref, count_ref, got_ref, other_ref, x_ref, w_ref, out_ref, held_ref):
@@ -435,7 +485,8 @@
     chip = chip_ref[0]
     flipped = lax.rem(chip, 2) == 1
     left = lax.broadcasted_iota(jnp.int32, (half, lanes), 1) < head_size
-    live = live_rows(count_ref[0], 2 * half, slot_rows, time_dev, lanes)
+    count = scalar(count_ref)
+    live = live_rows(count, 2 * half, slot_rows, time_dev, lanes)
     for slot in range(chips // 2):
         block = (slot + chip // 2) % (chips // 2) if chips == 4 else slot
         for side in range(2):
@@ -461,7 +512,7 @@
     mixed = jnp.dot(attended, w_ref[...], preferred_element_type=jnp.float32)
     full = x_ref[...].astype(jnp.float32) + mixed.reshape(time_dev, slots, width)
     slot = lax.broadcasted_iota(jnp.int32, full.shape, 1)
-    out_ref[...] = jnp.where(slot < count_ref[0], full, 0.0).astype(jnp.bfloat16)
+    out_ref[...] = jnp.where(slot < count, full, 0.0).astype(jnp.bfloat16)
 
 
 def mix(core, chip, count, got, other, tokens, w_out):
@@ -469,7 +520,7 @@
     return pl.pallas_call(
         mix_kernel,
         out_shape=jax.ShapeDtypeStruct(tokens.shape, jnp.bfloat16),
-        in_specs=[SMEM] * 3 + [VMEM] * 4,
+        in_specs=[SMEM] * 2 + [VMEM] * 5,
         out_specs=VMEM,
         scratch_shapes=[pltpu.VMEM((2 * half, w_out.shape[0]), jnp.bfloat16)],
         compiler_params=params(),
@@ -497,6 +548,7 @@
     chip = lax.axis_index("chip").reshape(1)
     by_time = jnp.transpose(tokens, (1, 0, 2))
     other_tokens = lax.ppermute(by_time, "core", SWAP)
+    tube_count = tube_count.reshape(1, 1)
     other_count = lax.ppermute(tube_count, "core", SWAP)
     fetched = fetch(core, by_time, ln_gain, ln_bias, w_qkv, rows)
     rows_in, gain, bias, weights = fetched
@@ -504,9 +556,9 @@
         chip, tube_count, other_count, rows_in, other_tokens, gain, bias, weights
     )
     got = spread(messages, chips)
-    least = up_to((HEADS - 1) * up_to(slot_rows, PACK) + rows, SIZE_STEP) + SIZE_STEP
-    most = up_to((HEADS - 1) * rows + up_to(slot_rows, PACK), SIZE_STEP)
-    sizes = list(range(least, most, SIZE_STEP))[:SIZE_CASES] + [most]
+    least = up_to((HEADS - 1) * slot_rows + rows, SIZE_STEP // 2)
+    most = up_to((HEADS - 1) * rows + slot_rows, SIZE_STEP)
+    sizes = [least + more for more in SIZES_ABOVE if least + more < most] + [most]
     kv, live, query, starts, case = pack(got, sizes, slot_rows, time_dev)
     branches = [functools.partial(attend_size, size, half) for size in sizes]
     returned = lax.switch(case[0], branches, kv, live, query, starts)

time: 56 us -> 51.5 us (0.920)
  starting transfers between devices: 19.2 us -> 14.9 us
  waiting for transfers between devices: 15.1 us -> 13.3 us
  Pallas kernels: 19.4 us -> 21.1 us
    ppermute x1, starting transfers between devices: 4.15 us -> 0.33 us  [exchange_and_attend(): far_late = lax.ppermute(second, 'far', SWAP)]
    ppermute x1, waiting for transfers between devices: 2.76 us -> 0.01 us  [exchange_and_attend(): near = lax.ppermute(both, 'near', SWAP)]
    ppermute x1, starting transfers between devices: 2.04 us -> 0.01 us  [exchange_and_attend(): both_late = lax.ppermute(far_late, 'near', SWAP)]
    pallas_call x5 -> x4, Pallas kernels: 14.6 us -> 16.2 us  [the longest x3 15.3 us: run_stage(): pl.pallas_call(functools.partial(attend_kernel, first, last, size, length...]
    ppermute x1, starting transfers between devices: 0.07 us -> 1.62 us  [exchange_and_attend(): both_early = lax.ppermute(far_early, 'near', SWAP)]
    ppermute x6, waiting for transfers between devices: 8.36 us -> 9.77 us  [spread(): lax.ppermute(arrays[hop], 'chip', [(i, i ^ hop) for i in range(chips)])]
    ppermute x1, waiting for transfers between devices: 2.67 us -> 1.59 us  [exchange_and_attend(): far_late = lax.ppermute(second, 'far', SWAP)]
    ppermute x1, waiting for transfers between devices: 0.01 us -> 0.7 us  [exchange_and_attend(): far_early = lax.ppermute(first, 'far', SWAP)]
  transfers between devices with their start and end apart: 14 -> 14, of which waited for: 8 -> 8; matrix products, arithmetic and copies ran while one was open for 0% -> 0% of each run, Pallas kernels for 20% -> 23%
where the time goes in v1:
time: 51.5 us; the launch traced here: 51.4 us
  Pallas kernels  21.1 us (41%)
  starting transfers between devices  14.9 us (29%)
  waiting for transfers between devices  13.3 us (26%)
  between operations  1.4 us (3%)
  loops' own time  0.53 us (1%)
    pallas_call x3, Pallas kernels, run_stage(): pl.pallas_call(functools.partial(attend_kernel, first, last, size, length...  15.3 us
    ppermute x6, waiting for transfers between devices, spread(): lax.ppermute(arrays[hop], 'chip', [(i, i ^ hop) for i in range(chips)])  9.77 us
    ppermute x6, starting transfers between devices, spread(): lax.ppermute(arrays[hop], 'chip', [(i, i ^ hop) for i in range(chips)])  8.12 us
    ppermute x1, starting transfers between devices, exchange_and_attend(): far_early = lax.ppermute(first, 'far', SWAP)  2.59 us
    pallas_call x1, Pallas kernels, project(): pl.pallas_call(project_kernel, out_shape=(message,) * chips, in_specs=[SM...  1.98 us
    ppermute x1, starting transfers between devices, exchange_and_attend(): near = lax.ppermute(both, 'near', SWAP)  1.64 us
    ppermute x1, starting transfers between devices, exchange_and_attend(): both_early = lax.ppermute(far_early, 'near', SWAP)  1.62 us
    ppermute x1, waiting for transfers between devices, exchange_and_attend(): far_late = lax.ppermute(second, 'far', SWAP)  1.59 us
  transfers between devices with their start and end apart: 14, of which 8 were waited for; matrix products, arithmetic and copies ran while one was open for 0% of the time, Pallas kernels for 23%

profile of v1, /device:TPU:0, one launch (start us, length us, event | category | flops | bytes accessed | tf_op | source)
XLA Modules:
  0.0 51.4 jit_solution(10424415374402494025)
XLA Ops:
  0.0 0.5 collective-permute-start.26
  0.5 0.0 collective-permute-start.25
  1.2 1.6 %fetch.1 = (bf16[160,1024]{1,0:T(8,128)(2,1)S(1)}, f32[1,1024]{1,0:T(1,128)S(1)}, f32[1,1024]{1,0:T(1,128)S(1)}, bf16[3,1024,256]{2,1,0:T(8,128)(2,1)S(1)}) custom-call(s32[1]{0:T(128)} %bitcast.core_ref, bf16[38,4,1024]{2,1,0:T(4,128)(2,1)} %bitcast.20, f32[1,1024]{1,0:T(1,128)} %bitcast.25, f32[1,1024]{1,0:T(1,128)} %bitcast.26, bf16[1024,1536]{1,0:T(8,128)(2,1)} %w_hbm.1), custom_call_target="tpu_custom_call" | custom-call | flops 503316480 | bytes 1572864 | tf_op jit(solution)/shard_map/fetch/pallas_call | solution.py:118
  2.7 0.0 collective-permute-done.25.other_count_ref
  2.7 2.0 %project.1 = (bf16[480,128]{1,0:T(8,128)(2,1)S(1)}, bf16[480,128]{1,0:T(8,128)(2,1)S(1)}, bf16[480,128]{1,0:T(8,128)(2,1)S(1)}, bf16[480,128]{1,0:T(8,128)(2,1)S(1)}) custom-call(s32[1]{0:T(128)} %bitcast.1.chip_ref, s32[1,1]{1,0:T(1,128)} %bitcast.17.count_ref, s32[1,1]{1,0:T(1,128)} %collective-permute-done.25.other_count_ref, ...), custom_call_target="tpu_custom_call" | custom-call | flops 503316480 | bytes 1572864 | tf_op jit(solution)/shard_map/project/pallas_call | solution.py:210
  4.7 3.0 %collective-permute-start.27 = (bf16[480,128]{1,0:T(8,128)(2,1)S(1)}, bf16[480,128]{1,0:T(8,128)(2,1)S(1)}, u32[]{:S(2)}, u32[]{:S(2)}) collective-permute-start(bf16[480,128]{1,0:T(8,128)(2,1)S(1)} %get-tuple-element.179), channel_id=1, source_target_pairs={{0,2},{2,0},{4,6},{6,4},{1,3},{3,1},{5,7},{7,5},{8,10},{10,8},{12,... | collective-permute-start | bytes 368648 | tf_op jit(solution)/shard_map/ppermute | solution.py:536
  7.8 1.5 %collective-permute-start.28 = (bf16[480,128]{1,0:T(8,128)(2,1)S(1)}, bf16[480,128]{1,0:T(8,128)(2,1)S(1)}, u32[]{:S(2)}, u32[]{:S(2)}) collective-permute-start(bf16[480,128]{1,0:T(8,128)(2,1)S(1)} %get-tuple-element.180), channel_id=1, source_target_pairs={{0,4},{2,6},{4,0},{6,2},{1,5},{3,7},{5,1},{7,3},{8,12},{10,14},{12... | collective-permute-start | bytes 368648 | tf_op jit(solution)/shard_map/ppermute | solution.py:536
  9.3 0.0 collective-permute-start.29
  9.3 2.2 %collective-permute-done.27.refs_1_ = bf16[480,128]{1,0:T(8,128)(2,1)S(1)} collective-permute-done((bf16[480,128]{1,0:T(8,128)(2,1)S(1)}, bf16[480,128]{1,0:T(8,128)(2,1)S(1)}, u32[]{:S(2)}, u32[]{:S(2)}) %collective-permute-start.27) | collective-permute-done | bytes 122912 | tf_op jit(solution)/shard_map/ppermute | solution.py:536
  11.5 3.9 %collective-permute-done.28.refs_2_ = bf16[480,128]{1,0:T(8,128)(2,1)S(1)} collective-permute-done((bf16[480,128]{1,0:T(8,128)(2,1)S(1)}, bf16[480,128]{1,0:T(8,128)(2,1)S(1)}, u32[]{:S(2)}, u32[]{:S(2)}) %collective-permute-start.28) | collective-permute-done | bytes 122912 | tf_op jit(solution)/shard_map/ppermute | solution.py:536
  15.4 0.9 %pack.1 = (bf16[1440,128]{1,0:T(8,128)(2,1)S(1)}, bf16[1440,128]{1,0:T(8,128)(2,1)S(1)}, bf16[1440,128]{1,0:T(8,128)(2,1)S(1)}, s32[9]{0:T(128)S(1)}, s32[1]{0:T(128)}) custom-call(bf16[480,128]{1,0:T(8,128)(2,1)S(1)} %get-tuple-element.178.refs_0_, bf16[480,128]{1,0:T(8,128)(2,1)S(1)} %collective-permute-done.27.refs_1_, ...), custom_call_target="tpu_custom_call" | custom-call | tf_op jit(solution)/shard_map/pack/pallas_call | solution.py:280
  16.9 0.0 copy-start
  16.9 0.0 copy-start.1
  16.9 24.4 %conditional.1 = (bf16[4,160,128]{2,1,0:T(8,128)(2,1)S(1)}) conditional(s32[]{:T(128)} %bitcast.6, (bf16[1440,128]{1,0:T(8,128)(2,1)S(1)}, s32[9]{0:T(128)S(1)}, bf16[1440,128]{1,0:T(8,128)(2,1)S(1)}, bf16[1440,128]{1,0:T(8,128)(2,1)S(1)}) %tuple.35, (bf16[1440,128]{1,0:T(8,128)(2,1)S(1)}, s32[9]{0:T(128)S(1)}, ...), branch_computations={%region_0.0_spmd, %region_1.0_spmd, %region_2.0_spmd, %region_3.0_... | conditional | flops 5033164800 | bytes 10485968 | solution.py:564
  17.2 1.6 %collective-permute-start.19 = (bf16[768,128]{1,0:T(8,128)(2,1)S(1)}, bf16[768,128]{1,0:T(8,128)(2,1)S(1)}, u32[]{:S(2)}, u32[]{:S(2)}) collective-permute-start(bf16[768,128]{1,0:T(8,128)(2,1)S(1)} %slice.50.refs_3_), channel_id=1, source_target_pairs={{0,8},{8,0},{1,9},{9,1},{2,10},{10,2},{3,11},{11,3},{4,12},{12,4},... | collective-permute-start | bytes 589832 | tf_op jit(solution)/shard_map/cond/branch_2_fun/ppermute | solution.py:466
  18.8 2.6 %collective-permute-start.15 = (bf16[384,128]{1,0:T(8,128)(2,1)S(1)}, bf16[384,128]{1,0:T(8,128)(2,1)S(1)}, u32[]{:S(2)}, u32[]{:S(2)}) collective-permute-start(bf16[384,128]{1,0:T(8,128)(2,1)S(1)} %get-tuple-element.99), channel_id=1, source_target_pairs={{0,16},{16,0},{1,17},{17,1},{2,18},{18,2},{3,19},{19,3},{4,20},{20... | collective-permute-start | bytes 294920 | tf_op jit(solution)/shard_map/cond/branch_2_fun/ppermute | solution.py:464
  21.4 0.3 collective-permute-start.17
  21.8 4.5 %branch_2_fun.3 = (f32[1440,128]{1,0:T(8,128)S(1)}, f32[1440,128]{1,0:T(8,128)S(1)}, f32[2]{0:T(128)S(1)}) custom-call(s32[9]{0:T(128)S(1)} %get-tuple-element.95.refs_0_, bf16[1440,128]{1,0:T(8,128)(2,1)S(1)} %get-tuple-element.96.refs_1_, bf16[1440,128]{1,0:T(8,128)(2,1)S(1)} %get-tuple-element.97.refs_2_, bf16[768,128]{1,0:T(8,128)(2,1)S(1)} %slice.50.refs_3_), custom_call_target="tpu_custom_call" | custom-call | flops 301989888 | bytes 786432 | tf_op jit(solution)/shard_map/cond/branch_2_fun/pallas_call | solution.py:436
  26.3 0.7 %collective-permute-done.15.refs_4_ = bf16[384,128]{1,0:T(8,128)(2,1)S(1)} collective-permute-done((bf16[384,128]{1,0:T(8,128)(2,1)S(1)}, bf16[384,128]{1,0:T(8,128)(2,1)S(1)}, u32[]{:S(2)}, u32[]{:S(2)}) %collective-permute-start.15) | collective-permute-done | bytes 98336 | tf_op jit(solution)/shard_map/cond/branch_2_fun/ppermute | solution.py:464
  27.0 1.6 %collective-permute-start.16 = (bf16[384,128]{1,0:T(8,128)(2,1)S(1)}, bf16[384,128]{1,0:T(8,128)(2,1)S(1)}, u32[]{:S(2)}, u32[]{:S(2)}) collective-permute-start(bf16[384,128]{1,0:T(8,128)(2,1)S(1)} %collective-permute-done.15.refs_4_), channel_id=1, source_target_pairs={{0,8},{8,0},{1,9},{9,1},{2,10},{10,2},{3,11},{11,3},{4,12},{12,4},... | collective-permute-start | bytes 294920 | tf_op jit(solution)/shard_map/cond/branch_2_fun/ppermute | solution.py:472
  28.6 1.6 %collective-permute-done.17.refs_5_ = bf16[384,128]{1,0:T(8,128)(2,1)S(1)} collective-permute-done((bf16[384,128]{1,0:T(8,128)(2,1)S(1)}, bf16[384,128]{1,0:T(8,128)(2,1)S(1)}, u32[]{:S(2)}, u32[]{:S(2)}) %collective-permute-start.17) | collective-permute-done | bytes 98336 | tf_op jit(solution)/shard_map/cond/branch_2_fun/ppermute | solution.py:465
  30.2 5.7 %branch_2_fun.4 = (f32[1440,128]{1,0:T(8,128)S(1)}, f32[1440,128]{1,0:T(8,128)S(1)}, f32[2]{0:T(128)S(1)}) custom-call(s32[9]{0:T(128)S(1)} %get-tuple-element.95.refs_0_, bf16[1440,128]{1,0:T(8,128)(2,1)S(1)} %get-tuple-element.96.refs_1_, bf16[1440,128]{1,0:T(8,128)(2,1)S(1)} %get-tuple-element.97.refs_2_, ...), custom_call_target="tpu_custom_call", output_to_operand_aliasing={{0}: (6, {}), {1}: (7, {})} | custom-call | flops 1207959552 | bytes 1572864 | tf_op jit(solution)/shard_map/cond/branch_2_fun/pallas_call | solution.py:436
  35.9 5.2 %branch_2_fun.5 = bf16[4,160,128]{2,1,0:T(8,128)(2,1)S(1)} custom-call(s32[9]{0:T(128)S(1)} %get-tuple-element.95.refs_0_, bf16[1440,128]{1,0:T(8,128)(2,1)S(1)} %get-tuple-element.96.refs_1_, bf16[1440,128]{1,0:T(8,128)(2,1)S(1)} %get-tuple-element.97.refs_2_, bf16[384,128]{1,0:T(8,128)(2,1)S(1)} %collective-permute-done.16.refs_3_, ...), custom_call_target="tpu_custom_call" | custom-call | flops 301989888 | bytes 786432 | tf_op jit(solution)/shard_map/cond/branch_2_fun/pallas_call | solution.py:436
  41.3 0.5 %collective-permute-start.31 = (bf16[160,128]{1,0:T(8,128)(2,1)S(1)}, bf16[160,128]{1,0:T(8,128)(2,1)S(1)}, u32[]{:S(2)}, u32[]{:S(2)}) collective-permute-start(bf16[160,128]{1,0:T(8,128)(2,1)S(1)} %get-tuple-element.195), channel_id=1, source_target_pairs={{0,4},{2,6},{4,0},{6,2},{1,5},{3,7},{5,1},{7,3},{8,12},{10,14},{12... | collective-permute-start | bytes 122888 | tf_op jit(solution)/shard_map/ppermute | solution.py:536
  41.9 2.7 %collective-permute-start.32 = (bf16[160,128]{1,0:T(8,128)(2,1)S(1)}, bf16[160,128]{1,0:T(8,128)(2,1)S(1)}, u32[]{:S(2)}, u32[]{:S(2)}) collective-permute-start(bf16[160,128]{1,0:T(8,128)(2,1)S(1)} %get-tuple-element.194), channel_id=1, source_target_pairs={{0,6},{2,4},{4,2},{6,0},{1,7},{3,5},{5,3},{7,1},{8,14},{10,12},{12... | collective-permute-start | bytes 122888 | tf_op jit(solution)/shard_map/ppermute | solution.py:536
  44.6 0.3 collective-permute-start.30
  44.9 0.5 collective-permute-done.31
  45.4 1.4 %collective-permute-done.32 = bf16[160,128]{1,0:T(8,128)(2,1)S(1)} collective-permute-done((bf16[160,128]{1,0:T(8,128)(2,1)S(1)}, bf16[160,128]{1,0:T(8,128)(2,1)S(1)}, u32[]{:S(2)}, u32[]{:S(2)}) %collective-permute-start.32) | collective-permute-done | bytes 40992 | tf_op jit(solution)/shard_map/ppermute | solution.py:536
  46.8 1.8 %collective-permute-done.30 = bf16[160,128]{1,0:T(8,128)(2,1)S(1)} collective-permute-done((bf16[160,128]{1,0:T(8,128)(2,1)S(1)}, bf16[160,128]{1,0:T(8,128)(2,1)S(1)}, u32[]{:S(2)}, u32[]{:S(2)}) %collective-permute-start.30) | collective-permute-done | bytes 40992 | tf_op jit(solution)/shard_map/ppermute | solution.py:536
  48.7 0.1 collective-permute-start.33
  48.7 1.3 %collective-permute-done.33.other_ref = bf16[4,80,128]{2,1,0:T(8,128)(2,1)S(1)} collective-permute-done((bf16[4,80,128]{2,1,0:T(8,128)(2,1)S(1)}, bf16[4,80,128]{2,1,0:T(8,128)(2,1)S(1)}, u32[]{:S(2)}, u32[]{:S(2)}) %collective-permute-start.33) | collective-permute-done | bytes 81952 | tf_op jit(solution)/shard_map/ppermute | solution.py:566
  50.0 1.4 %mix.1 = bf16[38,4,1024]{2,1,0:T(4,128)(2,1)} custom-call(s32[1]{0:T(128)} %bitcast.core_ref, s32[1]{0:T(128)} %bitcast.1.chip_ref, s32[1,1]{1,0:T(1,128)} %bitcast.18.count_ref, bf16[4,80,128]{2,1,0:T(8,128)(2,1)S(1)} %get-tuple-element.192.got_ref, bf16[4,80,128]{2,1,0:T(8,128)(2,1)S(1)} %collective-permute-done.33.other_ref, ...), custom_call_target="tpu_custom_call" | custom-call | flops 167772160 | bytes 1048576 | tf_op jit(solution)/shard_map/mix/pallas_call | solution.py:520
  (13 shorter events, 0.1 us)
Async XLA Ops:
  0.0 2.7 %collective-permute-start.26 = (bf16[38,4,1024]{2,1,0:T(4,128)(2,1)}, bf16[38,4,1024]{2,1,0:T(4,128)(2,1)S(1)}, u32[]{:S(2)}, u32[]{:S(2)}) collective-permute-start(bf16[38,4,1024]{2,1,0:T(4,128)(2,1)} %bitcast.19), channel_id=1, source_target_pairs={{0,1},{1,0},{2,3},{3,2},{4,5},{5,4},{6,7},{7,6},{8,9},{9,8},{10,11... | collective-permute-start | bytes 933896 | tf_op jit(solution)/shard_map/ppermute | solution.py:550
  0.5 2.2 %collective-permute-start.25 = (s32[1,1]{1,0:T(1,128)}, s32[1,1]{1,0:T(1,128)}, u32[]{:S(2)}, u32[]{:S(2)}) collective-permute-start(s32[1,1]{1,0:T(1,128)} %bitcast.2), channel_id=1, source_target_pairs={{0,1},{1,0},{2,3},{3,2},{4,5},{5,4},{6,7},{7,6},{8,9},{9,8},{10,11... | collective-permute-start | bytes 20 | tf_op jit(solution)/shard_map/ppermute | solution.py:552
  4.7 6.7 %collective-permute-start.27 = (bf16[480,128]{1,0:T(8,128)(2,1)S(1)}, bf16[480,128]{1,0:T(8,128)(2,1)S(1)}, u32[]{:S(2)}, u32[]{:S(2)}) collective-permute-start(bf16[480,128]{1,0:T(8,128)(2,1)S(1)} %get-tuple-element.179), channel_id=1, source_target_pairs={{0,2},{2,0},{4,6},{6,4},{1,3},{3,1},{5,7},{7,5},{8,10},{10,8},{12,... | collective-permute-start | bytes 368648 | tf_op jit(solution)/shard_map/ppermute | solution.py:536
  7.8 7.6 %collective-permute-start.28 = (bf16[480,128]{1,0:T(8,128)(2,1)S(1)}, bf16[480,128]{1,0:T(8,128)(2,1)S(1)}, u32[]{:S(2)}, u32[]{:S(2)}) collective-permute-start(bf16[480,128]{1,0:T(8,128)(2,1)S(1)} %get-tuple-element.180), channel_id=1, source_target_pairs={{0,4},{2,6},{4,0},{6,2},{1,5},{3,7},{5,1},{7,3},{8,12},{10,14},{12... | collective-permute-start | bytes 368648 | tf_op jit(solution)/shard_map/ppermute | solution.py:536
  9.3 6.1 %collective-permute-start.29 = (bf16[480,128]{1,0:T(8,128)(2,1)S(1)}, bf16[480,128]{1,0:T(8,128)(2,1)S(1)}, u32[]{:S(2)}, u32[]{:S(2)}) collective-permute-start(bf16[480,128]{1,0:T(8,128)(2,1)S(1)} %get-tuple-element.181), channel_id=1, source_target_pairs={{0,6},{2,4},{4,2},{6,0},{1,7},{3,5},{5,3},{7,1},{8,14},{10,12},{12... | collective-permute-start | bytes 368648 | tf_op jit(solution)/shard_map/ppermute | solution.py:536
  16.9 33.1 %copy-start = (bf16[4,38,1024]{2,0,1:T(4,128)(2,1)S(1)}, bf16[4,38,1024]{2,0,1:T(4,128)(2,1)}, u32[]{:S(2)}) copy-start(bf16[4,38,1024]{2,0,1:T(4,128)(2,1)} %param.11) | copy-start | bytes 933892
  16.9 33.1 %copy-start.1 = (bf16[512,1024]{1,0:T(8,128)(2,1)S(1)}, bf16[512,1024]{1,0:T(8,128)(2,1)}, u32[]{:S(2)}) copy-start(bf16[512,1024]{1,0:T(8,128)(2,1)} %w_ref.1) | copy-start | bytes 3145732
  17.2 13.0 %collective-permute-start.19 = (bf16[768,128]{1,0:T(8,128)(2,1)S(1)}, bf16[768,128]{1,0:T(8,128)(2,1)S(1)}, u32[]{:S(2)}, u32[]{:S(2)}) collective-permute-start(bf16[768,128]{1,0:T(8,128)(2,1)S(1)} %slice.50.refs_3_), channel_id=1, source_target_pairs={{0,8},{8,0},{1,9},{9,1},{2,10},{10,2},{3,11},{11,3},{4,12},{12,4},... | collective-permute-start | bytes 589832 | tf_op jit(solution)/shard_map/cond/branch_2_fun/ppermute | solution.py:466
  18.8 8.1 %collective-permute-start.15 = (bf16[384,128]{1,0:T(8,128)(2,1)S(1)}, bf16[384,128]{1,0:T(8,128)(2,1)S(1)}, u32[]{:S(2)}, u32[]{:S(2)}) collective-permute-start(bf16[384,128]{1,0:T(8,128)(2,1)S(1)} %get-tuple-element.99), channel_id=1, source_target_pairs={{0,16},{16,0},{1,17},{17,1},{2,18},{18,2},{3,19},{19,3},{4,20},{20... | collective-permute-start | bytes 294920 | tf_op jit(solution)/shard_map/cond/branch_2_fun/ppermute | solution.py:464
  21.4 8.7 %collective-permute-start.17 = (bf16[384,128]{1,0:T(8,128)(2,1)S(1)}, bf16[384,128]{1,0:T(8,128)(2,1)S(1)}, u32[]{:S(2)}, u32[]{:S(2)}) collective-permute-start(bf16[384,128]{1,0:T(8,128)(2,1)S(1)} %get-tuple-element.105), channel_id=1, source_target_pairs={{0,16},{16,0},{1,17},{17,1},{2,18},{18,2},{3,19},{19,3},{4,20},{20... | collective-permute-start | bytes 294920 | tf_op jit(solution)/shard_map/cond/branch_2_fun/ppermute | solution.py:465
  27.0 8.9 %collective-permute-start.16 = (bf16[384,128]{1,0:T(8,128)(2,1)S(1)}, bf16[384,128]{1,0:T(8,128)(2,1)S(1)}, u32[]{:S(2)}, u32[]{:S(2)}) collective-permute-start(bf16[384,128]{1,0:T(8,128)(2,1)S(1)} %collective-permute-done.15.refs_4_), channel_id=1, source_target_pairs={{0,8},{8,0},{1,9},{9,1},{2,10},{10,2},{3,11},{11,3},{4,12},{12,4},... | collective-permute-start | bytes 294920 | tf_op jit(solution)/shard_map/cond/branch_2_fun/ppermute | solution.py:472
  30.2 5.7 %collective-permute-start.18 = (bf16[384,128]{1,0:T(8,128)(2,1)S(1)}, bf16[384,128]{1,0:T(8,128)(2,1)S(1)}, u32[]{:S(2)}, u32[]{:S(2)}) collective-permute-start(bf16[384,128]{1,0:T(8,128)(2,1)S(1)} %collective-permute-done.17.refs_5_), channel_id=1, source_target_pairs={{0,8},{8,0},{1,9},{9,1},{2,10},{10,2},{3,11},{11,3},{4,12},{12,4},... | collective-permute-start | bytes 294920 | tf_op jit(solution)/shard_map/cond/branch_2_fun/ppermute | solution.py:473
  41.3 4.1 %collective-permute-start.31 = (bf16[160,128]{1,0:T(8,128)(2,1)S(1)}, bf16[160,128]{1,0:T(8,128)(2,1)S(1)}, u32[]{:S(2)}, u32[]{:S(2)}) collective-permute-start(bf16[160,128]{1,0:T(8,128)(2,1)S(1)} %get-tuple-element.195), channel_id=1, source_target_pairs={{0,4},{2,6},{4,0},{6,2},{1,5},{3,7},{5,1},{7,3},{8,12},{10,14},{12... | collective-permute-start | bytes 122888 | tf_op jit(solution)/shard_map/ppermute | solution.py:536
  41.9 4.9 %collective-permute-start.32 = (bf16[160,128]{1,0:T(8,128)(2,1)S(1)}, bf16[160,128]{1,0:T(8,128)(2,1)S(1)}, u32[]{:S(2)}, u32[]{:S(2)}) collective-permute-start(bf16[160,128]{1,0:T(8,128)(2,1)S(1)} %get-tuple-element.194), channel_id=1, source_target_pairs={{0,6},{2,4},{4,2},{6,0},{1,7},{3,5},{5,3},{7,1},{8,14},{10,12},{12... | collective-permute-start | bytes 122888 | tf_op jit(solution)/shard_map/ppermute | solution.py:536
  44.6 4.0 %collective-permute-start.30 = (bf16[160,128]{1,0:T(8,128)(2,1)S(1)}, bf16[160,128]{1,0:T(8,128)(2,1)S(1)}, u32[]{:S(2)}, u32[]{:S(2)}) collective-permute-start(bf16[160,128]{1,0:T(8,128)(2,1)S(1)} %get-tuple-element.196), channel_id=1, source_target_pairs={{0,2},{2,0},{4,6},{6,4},{1,3},{3,1},{5,7},{7,5},{8,10},{10,8},{12,... | collective-permute-start | bytes 122888 | tf_op jit(solution)/shard_map/ppermute | solution.py:536
  48.7 1.3 %collective-permute-start.33 = (bf16[4,80,128]{2,1,0:T(8,128)(2,1)S(1)}, bf16[4,80,128]{2,1,0:T(8,128)(2,1)S(1)}, u32[]{:S(2)}, u32[]{:S(2)}) collective-permute-start(bf16[4,80,128]{2,1,0:T(8,128)(2,1)S(1)} %get-tuple-element.191), channel_id=1, source_target_pairs={{0,1},{1,0},{2,3},{3,2},{4,5},{5,4},{6,7},{7,6},{8,9},{9,8},{10,11... | collective-permute-start | bytes 245768 | tf_op jit(solution)/shard_map/ppermute | solution.py:566
